TPU v7x, 256 devices: a whole 4x4x8 slice. The times are simulated.
256 devices in a mesh: scen: 16 (over z, y_hi), gen: 16 (over y_lo, x, core).
Axes of the slice: x: 4, y: 4 (y_hi: 2, y_lo: 2; y = y_hi * 2 + y_lo), z: 8, core: 2. Of those that a mesh axis runs over, the one named last changes fastest.
Arguments:
- zone_load: float32 [256, 16, 256], P('scen'), may hold values from 0.3 to 1
- linear_cost: float32 [16, 20480], P(None, 'gen'), may hold values from -4 to 4
- cost_diag: float32 [20480], P('gen'), may hold values from 0.5 to 2
- capacity: float32 [20480], P('gen'), may hold values from 0.5 to 2
- cost_tiles: bfloat16 [80, 256, 256], P('gen'), may hold values from -0.375 to 0.375
- coupling_tiles: bfloat16 [16, 80, 256, 256], P('scen', 'gen'), may hold values from -0.375 to 0.375
- block_map: int32 [16, 80], P('scen', 'gen'), may hold values 0 or 1
- zone_index: int32 [20480], P('gen'), may hold values from 0 to 255
- step_numer: int32 [5], replicated, may hold values from 1 to 4
- step_denom: int32 [5], replicated, may hold values from 5 to 8
Outputs:
- dispatch: float32 [256, 16, 20480], P('scen', None, 'gen')
- prices: float32 [256, 16, 256], P('scen')
- plan: float32 [16, 20480], P(None, 'gen')
All inputs are finite; a program needn't handle non-finite values. No bound on the sum of `block_map` on one device may be relied on, other than what follows from the above.
Results may differ from a plain program's by a relative error of at most 0.0003.
Values sent between devices are 32-bit elements; how exact they have to be, the bound alone decides.
A program may use at most 64 MiB of HBM per device.

v0:
```python
import jax
import jax.numpy as jnp
from jax import lax
from jax.sharding import Mesh
from jax.sharding import PartitionSpec as P

G = 20480
ITERS = 5
GEN = ("gen_0", "gen_1", "gen_2")
SCEN = ("scen_0", "scen_1")
SCEN_GEN = ("scen_0", "scen_1", "gen_0", "gen_1", "gen_2")


penalty = 2.0
centering = 0.5
epsilon = 1e-06


def copy_for_each(value, axis):
    copies = jnp.broadcast_to(value, (lax.axis_size(axis), *value.shape))
    return lax.all_to_all(copies, axis, split_axis=0, concat_axis=0, tiled=True)


def taken_together(value, axis):
    return copy_for_each(value, axis).sum(axis=0)


def over_pieces(value, axis):
    blocks = lax.all_gather(value, axis)
    return blocks.sum(axis=0)


def by_axis(value, axes):
    for axis in axes:
        value = lax.psum(value, axis)
    return value


def local(
    zone_load,
    linear_cost,
    cost_diag,
    capacity,
    cost_tiles,
    coupling_tiles,
    block_map,
    zone_index,
    step_numer,
    step_denom,
):
    local_scen = zone_load.shape[0]
    periods = linear_cost.shape[0]
    zone_count = zone_load.shape[2]
    local_gen = capacity.shape[0]
    local_blocks = cost_tiles.shape[0]
    tile_width = cost_tiles.shape[2]
    gen_devices = lax.axis_size(GEN)
    total_scen = local_scen * lax.axis_size(SCEN)
    row_count = local_scen * periods
    entries = float(total_scen * periods * G)
    coupling = coupling_tiles[0]
    block_mask = block_map[0].astype(jnp.float32)
    onehot = (zone_index[:, None] == jnp.arange(zone_count, dtype=jnp.int32)[None, :]).astype(
        jnp.float32
    )
    scen_ids = lax.axis_index(SCEN) * local_scen + jnp.arange(local_scen, dtype=jnp.int32)
    levels = 0.2 + 0.6 * (scen_ids.astype(jnp.float32) + 0.5) / total_scen
    dispatch = jnp.broadcast_to(levels[:, None, None] * capacity, (local_scen, periods, local_gen))
    low_dual = jnp.ones((local_scen, periods, local_gen), jnp.float32)
    high_dual = jnp.ones((local_scen, periods, local_gen), jnp.float32)
    prices = jnp.zeros((local_scen, periods, zone_count), jnp.float32)
    lowest = 0.02 * capacity
    highest = 0.98 * capacity
    plan = jnp.zeros((periods, local_gen), jnp.float32)
    for iteration in range(ITERS):
        step_size = step_numer[iteration].astype(jnp.float32) / step_denom[iteration].astype(
            jnp.float32
        )
        column_sums = taken_together(jnp.sum(dispatch, axis=0), SCEN)
        plan = column_sums / total_scen
        partial_value = jnp.dot(
            dispatch.reshape(row_count, local_gen),
            onehot,
            precision=lax.Precision.HIGHEST,
            preferred_element_type=jnp.float32,
        )
        totals = over_pieces(partial_value, GEN)
        imbalance = totals.reshape(local_scen, periods, zone_count) * (zone_count / G) - zone_load
        primal_local = jnp.sum(imbalance * imbalance) / gen_devices
        rounded = dispatch.astype(jnp.bfloat16).reshape(row_count, local_blocks, tile_width)
        cross_part = jnp.einsum(
            "rki,kij->rkj", rounded, coupling, preferred_element_type=jnp.float32
        )
        own_part = jnp.einsum(
            "rki,kij->rkj", rounded, cost_tiles, preferred_element_type=jnp.float32
        )
        products = (own_part + cross_part * block_mask[None, :, None]).reshape(
            local_scen, periods, local_gen
        )
        price_terms = jnp.dot(
            prices.reshape(row_count, zone_count),
            onehot.T,
            precision=lax.Precision.HIGHEST,
            preferred_element_type=jnp.float32,
        )
        residual = (
            cost_diag * dispatch
            + products
            + linear_cost
            + penalty * (dispatch - plan)
            + price_terms.reshape(local_scen, periods, local_gen)
            - low_dual
            + high_dual
        )
        gap_local = jnp.sum(dispatch * low_dual + (capacity - dispatch) * high_dual)
        dual_local = jnp.sum(residual * residual)
        stacked = jnp.stack([gap_local, dual_local, primal_local])
        summed = by_axis(stacked, SCEN_GEN)
        gap_sum = summed[0]
        dual_sq = summed[1]
        primal_sq = summed[2]
        target = centering * gap_sum / (2.0 * entries)
        dual_rms = jnp.sqrt(dual_sq / entries + epsilon)
        primal_rms = jnp.sqrt(primal_sq / float(total_scen * periods * zone_count) + epsilon)
        scaling = cost_diag + penalty + low_dual / dispatch + high_dual / (capacity - dispatch)
        updated = jnp.clip(
            dispatch - step_size * residual / (scaling * (1.0 + dual_rms)), lowest, highest
        )
        low_dual = low_dual + step_size * (target / updated - low_dual)
        high_dual = high_dual + step_size * (target / (capacity - updated) - high_dual)
        prices = prices + step_size * imbalance / (1.0 + primal_rms)
        dispatch = updated
    return (dispatch, prices, plan)


def solution(mesh):
    torus = Mesh(
        mesh.devices.reshape(8, 2, 2, 4, 2), ("scen_0", "scen_1", "gen_0", "gen_1", "gen_2")
    )
    placed = (
        P(SCEN, None, None),
        P(None, GEN),
        P(GEN),
        P(GEN),
        P(GEN, None, None),
        P(SCEN, GEN, None, None),
        P(SCEN, GEN),
        P(GEN),
        P(),
        P(),
    )
    return jax.shard_map(
        local,
        mesh=torus,
        in_specs=placed,
        out_specs=(P(SCEN, None, GEN), P(SCEN, None, None), P(None, GEN)),
        check_vma=False,
    )
```

profile of v0, /device:TPU:1, one launch (start us, length us, event | category | flops | bytes accessed | tf_op | source)
XLA Modules:
  0.0 563.9 jit_solution(9734501786071534831)
XLA Ops:
  11.2 11.8 %all-to-all-start = ((f32[16,16,1280]{2,1,0:T(8,128)}), f32[16,16,1280]{2,1,0:T(8,128)}, u32[]{:S(2)}, u32[]{:S(2)}) async-start(f32[16,16,1280]{2,1,0:T(8,128)} %broadcast_in_dim.30), calls=%async_computation | async-start | bytes 2621440 | tf_op jit(solution)/shard_map/all_to_all | solution.py:21
  25.3 2.1 copy.38
  30.3 24.3 %all-to-all-done = f32[16,16,1280]{2,1,0:T(8,128)} async-done(((f32[16,16,1280]{2,1,0:T(8,128)}), f32[16,16,1280]{2,1,0:T(8,128)}, u32[]{:S(2)}, u32[]{:S(2)}) %all-to-all-start) | async-done | bytes 1310752 | tf_op jit(solution)/shard_map/all_to_all | solution.py:21
  56.0 2.7 multiply_reduce_fusion.4
  58.7 6.3 %all-gather.11.cloned.1.call-done = f32[4096,256]{1,0:T(8,128)} async-done(((f32[256,256]{1,0:T(8,128)}), f32[4096,256]{1,0:T(8,128)}) %all-gather.11.cloned.1.call-update) | async-done | bytes 4194320 | tf_op jit(solution)/shard_map/all_gather | solution.py:29
  65.0 2.5 reduce_sum.274
  70.8 14.7 %psum.175 = f32[3]{0:T(128)S(1)} all-reduce(f32[3]{0:T(128)S(1)} %pad_maximum_fusion), channel_id=1, replica_groups=mesh['scen_0'=8,'scen_1'=2,'gen_0'=2,'gen_1'=4,'gen_2'=2] {'scen_0'}, use_global_device_ids=true, to_apply=%region_6.0 | all-reduce | flops 3 | bytes 24 | tf_op jit(solution)/shard_map/psum | solution.py:35
  86.1 5.3 psum.176
  92.0 4.1 psum.177
  96.8 7.0 %psum.178 = f32[3]{0:T(128)S(1)} all-reduce(f32[3]{0:T(128)S(1)} %psum.177), channel_id=1, replica_groups=mesh['scen_0'=8,'scen_1'=2,'gen_0'=2,'gen_1'=4,'gen_2'=2] {'gen_1'}, use_global_device_ids=true, to_apply=%region_9.0 | all-reduce | flops 3 | bytes 24 | tf_op jit(solution)/shard_map/psum | solution.py:35
  103.8 10.2 %psum.179 = f32[3]{0:T(128)S(1)} all-reduce(f32[3]{0:T(128)S(1)} %psum.178), channel_id=1, replica_groups=mesh['scen_0'=8,'scen_1'=2,'gen_0'=2,'gen_1'=4,'gen_2'=2] {'gen_2'}, use_global_device_ids=true, to_apply=%region_10.0 | all-reduce | flops 3 | bytes 24 | tf_op jit(solution)/shard_map/psum | solution.py:35
  115.9 2.9 add_reduce_fusion.3
  121.7 6.3 %all-to-all-start.1 = ((f32[16,16,1280]{2,1,0:T(8,128)}), f32[16,16,1280]{2,1,0:T(8,128)}, u32[]{:S(2)}, u32[]{:S(2)}) async-start(f32[16,16,1280]{2,1,0:T(8,128)} %broadcast_in_dim.32), calls=%async_computation.1 | async-start | bytes 2621440 | tf_op jit(solution)/shard_map/all_to_all | solution.py:21
  133.2 2.1 copy.41
  137.2 22.7 %all-to-all-done.1 = f32[16,16,1280]{2,1,0:T(8,128)} async-done(((f32[16,16,1280]{2,1,0:T(8,128)}), f32[16,16,1280]{2,1,0:T(8,128)}, u32[]{:S(2)}, u32[]{:S(2)}) %all-to-all-start.1) | async-done | bytes 1310752 | tf_op jit(solution)/shard_map/all_to_all | solution.py:21
  162.8 4.6 multiply_reduce_fusion.3
  167.4 2.5 reduce_sum.280
  172.5 14.5 %psum.180 = f32[3]{0:T(128)S(1)} all-reduce(f32[3]{0:T(128)S(1)} %pad_maximum_fusion.1), channel_id=1, replica_groups=mesh['scen_0'=8,'scen_1'=2,'gen_0'=2,'gen_1'=4,'gen_2'=2] {'scen_0'}, use_global_device_ids=true, to_apply=%region_17.18 | all-reduce | flops 3 | bytes 24 | tf_op jit(solution)/shard_map/psum | solution.py:35
  186.9 5.3 psum.181
  192.9 4.1 psum.182
  197.6 6.3 %psum.183 = f32[3]{0:T(128)S(1)} all-reduce(f32[3]{0:T(128)S(1)} %psum.182), channel_id=1, replica_groups=mesh['scen_0'=8,'scen_1'=2,'gen_0'=2,'gen_1'=4,'gen_2'=2] {'gen_1'}, use_global_device_ids=true, to_apply=%region_20.21 | all-reduce | flops 3 | bytes 24 | tf_op jit(solution)/shard_map/psum | solution.py:35
  204.0 10.3 %psum.184 = f32[3]{0:T(128)S(1)} all-reduce(f32[3]{0:T(128)S(1)} %psum.183), channel_id=1, replica_groups=mesh['scen_0'=8,'scen_1'=2,'gen_0'=2,'gen_1'=4,'gen_2'=2] {'gen_2'}, use_global_device_ids=true, to_apply=%region_21.22 | all-reduce | flops 3 | bytes 24 | tf_op jit(solution)/shard_map/psum | solution.py:35
  216.3 3.9 add_reduce_fusion.2
  223.9 6.5 %all-to-all-start.2 = ((f32[16,16,1280]{2,1,0:T(8,128)}), f32[16,16,1280]{2,1,0:T(8,128)}, u32[]{:S(2)}, u32[]{:S(2)}) async-start(f32[16,16,1280]{2,1,0:T(8,128)} %broadcast_in_dim.33), calls=%async_computation.2 | async-start | bytes 2621440 | tf_op jit(solution)/shard_map/all_to_all | solution.py:21
  232.3 2.5 reshape.274
  237.0 2.1 copy.44
  239.1 2.7 reshape.275
  241.9 20.4 %all-to-all-done.2 = f32[16,16,1280]{2,1,0:T(8,128)} async-done(((f32[16,16,1280]{2,1,0:T(8,128)}), f32[16,16,1280]{2,1,0:T(8,128)}, u32[]{:S(2)}, u32[]{:S(2)}) %all-to-all-start.2) | async-done | bytes 1310752 | tf_op jit(solution)/shard_map/all_to_all | solution.py:21
  265.8 2.7 all-gather.15.cloned.1.call-done
  268.5 3.2 reduce_sum.286
  272.7 2.5 divide_add_fusion.3
  275.8 5.3 multiply_reduce_fusion.2
  282.3 14.7 %psum.185 = f32[3]{0:T(128)S(1)} all-reduce(f32[3]{0:T(128)S(1)} %pad_maximum_fusion.2), channel_id=1, replica_groups=mesh['scen_0'=8,'scen_1'=2,'gen_0'=2,'gen_1'=4,'gen_2'=2] {'scen_0'}, use_global_device_ids=true, to_apply=%region_28.29 | all-reduce | flops 3 | bytes 24 | tf_op jit(solution)/shard_map/psum | solution.py:35
  297.1 5.3 psum.186
  303.0 4.0 psum.187
  307.7 6.7 %psum.188 = f32[3]{0:T(128)S(1)} all-reduce(f32[3]{0:T(128)S(1)} %psum.187), channel_id=1, replica_groups=mesh['scen_0'=8,'scen_1'=2,'gen_0'=2,'gen_1'=4,'gen_2'=2] {'gen_1'}, use_global_device_ids=true, to_apply=%region_31.32 | all-reduce | flops 3 | bytes 24 | tf_op jit(solution)/shard_map/psum | solution.py:35
  314.4 10.2 %psum.189 = f32[3]{0:T(128)S(1)} all-reduce(f32[3]{0:T(128)S(1)} %psum.188), channel_id=1, replica_groups=mesh['scen_0'=8,'scen_1'=2,'gen_0'=2,'gen_1'=4,'gen_2'=2] {'gen_2'}, use_global_device_ids=true, to_apply=%region_32.33 | all-reduce | flops 3 | bytes 24 | tf_op jit(solution)/shard_map/psum | solution.py:35
  326.6 5.3 add_reduce_fusion.1
  334.8 6.7 %all-to-all-start.3 = ((f32[16,16,1280]{2,1,0:T(8,128)}), f32[16,16,1280]{2,1,0:T(8,128)}, u32[]{:S(2)}, u32[]{:S(2)}) async-start(f32[16,16,1280]{2,1,0:T(8,128)} %broadcast_in_dim.34), calls=%async_computation.3 | async-start | bytes 2621440 | tf_op jit(solution)/shard_map/all_to_all | solution.py:21
  346.6 2.1 copy.47
  348.8 2.7 reshape.278
  351.5 21.8 %all-to-all-done.3 = f32[16,16,1280]{2,1,0:T(8,128)} async-done(((f32[16,16,1280]{2,1,0:T(8,128)}), f32[16,16,1280]{2,1,0:T(8,128)}, u32[]{:S(2)}, u32[]{:S(2)}) %all-to-all-start.3) | async-done | bytes 1310752 | tf_op jit(solution)/shard_map/all_to_all | solution.py:21
  376.2 4.8 multiply_reduce_fusion.1
  381.0 3.2 reduce_sum.292
  388.4 15.2 %psum.190 = f32[3]{0:T(128)} all-reduce(f32[3]{0:T(128)} %pad_maximum_fusion.3), channel_id=1, replica_groups=mesh['scen_0'=8,'scen_1'=2,'gen_0'=2,'gen_1'=4,'gen_2'=2] {'scen_0'}, use_global_device_ids=true, to_apply=%region_39.40 | all-reduce | flops 3 | bytes 24 | tf_op jit(solution)/shard_map/psum | solution.py:35
  403.5 5.9 %psum.191 = f32[3]{0:T(128)} all-reduce(f32[3]{0:T(128)} %psum.190), channel_id=1, replica_groups=mesh['scen_0'=8,'scen_1'=2,'gen_0'=2,'gen_1'=4,'gen_2'=2] {'scen_1'}, use_global_device_ids=true, to_apply=%region_40.41 | all-reduce | flops 3 | bytes 24 | tf_op jit(solution)/shard_map/psum | solution.py:35
  410.1 4.6 psum.192
  415.3 7.4 %psum.193 = f32[3]{0:T(128)} all-reduce(f32[3]{0:T(128)} %psum.192), channel_id=1, replica_groups=mesh['scen_0'=8,'scen_1'=2,'gen_0'=2,'gen_1'=4,'gen_2'=2] {'gen_1'}, use_global_device_ids=true, to_apply=%region_42.43 | all-reduce | flops 3 | bytes 24 | tf_op jit(solution)/shard_map/psum | solution.py:35
  422.7 11.7 %psum.194 = f32[3]{0:T(128)} all-reduce(f32[3]{0:T(128)} %psum.193), channel_id=1, replica_groups=mesh['scen_0'=8,'scen_1'=2,'gen_0'=2,'gen_1'=4,'gen_2'=2] {'gen_2'}, use_global_device_ids=true, to_apply=%region_43.44 | all-reduce | flops 3 | bytes 24 | tf_op jit(solution)/shard_map/psum | solution.py:35
  437.0 3.8 add_reduce_fusion
  444.8 6.1 %all-to-all-start.4 = ((f32[16,16,1280]{2,1,0:T(8,128)}), f32[16,16,1280]{2,1,0:T(8,128)}, u32[]{:S(2)}, u32[]{:S(2)}) async-start(f32[16,16,1280]{2,1,0:T(8,128)} %broadcast_in_dim.35), calls=%async_computation.4 | async-start | bytes 2621440 | tf_op jit(solution)/shard_map/all_to_all | solution.py:21
  455.6 2.1 copy.50
  457.8 2.8 reshape.281
  460.6 22.0 %all-to-all-done.4 = f32[16,16,1280]{2,1,0:T(8,128)} async-done(((f32[16,16,1280]{2,1,0:T(8,128)}), f32[16,16,1280]{2,1,0:T(8,128)}, u32[]{:S(2)}, u32[]{:S(2)}) %all-to-all-start.4) | async-done | bytes 1310752 | tf_op jit(solution)/shard_map/all_to_all | solution.py:21
  484.6 4.8 all-gather.19.cloned.1.call-done
  489.4 3.2 reduce_sum.298
  493.7 2.6 multiply_reduce_fusion.5
  496.9 5.0 multiply_reduce_fusion
  503.8 15.3 %psum.195 = f32[3]{0:T(128)} all-reduce(f32[3]{0:T(128)} %pad_maximum_fusion.4), channel_id=1, replica_groups=mesh['scen_0'=8,'scen_1'=2,'gen_0'=2,'gen_1'=4,'gen_2'=2] {'scen_0'}, use_global_device_ids=true, to_apply=%region_50.51 | all-reduce | flops 3 | bytes 24 | tf_op jit(solution)/shard_map/psum | solution.py:35
  519.1 5.9 %psum.196 = f32[3]{0:T(128)} all-reduce(f32[3]{0:T(128)} %psum.195), channel_id=1, replica_groups=mesh['scen_0'=8,'scen_1'=2,'gen_0'=2,'gen_1'=4,'gen_2'=2] {'scen_1'}, use_global_device_ids=true, to_apply=%region_51.52 | all-reduce | flops 3 | bytes 24 | tf_op jit(solution)/shard_map/psum | solution.py:35
  525.6 4.4 psum.197
  530.6 7.1 %psum.198 = f32[3]{0:T(128)} all-reduce(f32[3]{0:T(128)} %psum.197), channel_id=1, replica_groups=mesh['scen_0'=8,'scen_1'=2,'gen_0'=2,'gen_1'=4,'gen_2'=2] {'gen_1'}, use_global_device_ids=true, to_apply=%region_53.54 | all-reduce | flops 3 | bytes 24 | tf_op jit(solution)/shard_map/psum | solution.py:35
  537.7 11.1 %psum.199 = f32[3]{0:T(128)} all-reduce(f32[3]{0:T(128)} %psum.198), channel_id=1, replica_groups=mesh['scen_0'=8,'scen_1'=2,'gen_0'=2,'gen_1'=4,'gen_2'=2] {'gen_2'}, use_global_device_ids=true, to_apply=%region_54.55 | all-reduce | flops 3 | bytes 24 | tf_op jit(solution)/shard_map/psum | solution.py:35
  553.4 3.7 maximum_minimum_fusion
  (152 shorter events, 73.7 us)
Async XLA Ops:
  7.2 16.7 %copy-start = (bf16[5,256,256]{2,1,0:T(8,128)(2,1)S(1)}, bf16[5,256,256]{2,1,0:T(8,128)(2,1)}, u32[]{:S(2)}) copy-start(bf16[5,256,256]{2,1,0:T(8,128)(2,1)} %param.14) | copy-start | bytes 1966084
  7.2 1.0 copy-start.21
  7.2 57.8 %all-gather.11.cloned.1.call-start = ((), (), s32[]{:S(2)}) async-start(), calls=%async_computation.5 | async-start | bytes 4456448 | tf_op jit(solution)/shard_map/all_gather | solution.py:29
  8.1 1.8 copy-start.16
  11.2 43.4 %all-to-all-start = ((f32[16,16,1280]{2,1,0:T(8,128)}), f32[16,16,1280]{2,1,0:T(8,128)}, u32[]{:S(2)}, u32[]{:S(2)}) async-start(f32[16,16,1280]{2,1,0:T(8,128)} %broadcast_in_dim.30), calls=%async_computation | async-start | bytes 2621440 | tf_op jit(solution)/shard_map/all_to_all | solution.py:21
  23.0 0.8 copy-start.34
  23.0 144.4 %all-gather.13.cloned.1.call-start = ((), (), s32[]{:S(2)}) async-start(), calls=%async_computation.6 | async-start | bytes 4456448 | tf_op jit(solution)/shard_map/all_gather | solution.py:29
  23.8 1.5 copy-start.27
  23.9 1.1 copy-start.6
  27.5 2.8 copy-start.26
  29.4 26.7 %copy-start.25 = (f32[16,1280]{1,0:T(8,128)S(1)}, f32[16,1280]{1,0:T(8,128)}, u32[]{:S(2)}) copy-start(f32[16,1280]{1,0:T(8,128)} %param.11) | copy-start | bytes 245764
  30.3 85.6 %copy-start.19 = (f32[1280]{0:T(1024)}, f32[1280]{0:T(1024)S(1)}, u32[]{:S(2)}) copy-start(f32[1280]{0:T(1024)S(1)} %get-tuple-element.24) | copy-start | bytes 15364
  30.3 85.6 %copy-start.20 = (f32[1280]{0:T(1024)}, f32[1280]{0:T(1024)S(1)}, u32[]{:S(2)}) copy-start(f32[1280]{0:T(1024)S(1)} %get-tuple-element.25) | copy-start | bytes 15364
  65.0 2.6 copy-start.10
  65.0 5.2 copy-start.32
  65.0 20.5 %copy-start.33 = (s32[5]{0:T(128)S(1)}, s32[5]{0:T(128)}, u32[]{:S(2)}) copy-start(s32[5]{0:T(128)} %param.19) | copy-start | bytes 64
  67.5 48.4 %copy-start.13 = (f32[256,256]{1,0:T(8,128)}, f32[256,256]{1,0:T(8,128)S(1)}, u32[]{:S(2)}) copy-start(f32[256,256]{1,0:T(8,128)S(1)} %reduce_sum.274) | copy-start | bytes 786436
  67.5 48.3 %copy-start.15 = (f32[256,256]{1,0:T(8,128)}, f32[256,256]{1,0:T(8,128)S(1)}, u32[]{:S(2)}) copy-start(f32[256,256]{1,0:T(8,128)S(1)} %broadcast_multiply_fusion.4) | copy-start | bytes 786436
  121.7 38.1 %all-to-all-start.1 = ((f32[16,16,1280]{2,1,0:T(8,128)}), f32[16,16,1280]{2,1,0:T(8,128)}, u32[]{:S(2)}, u32[]{:S(2)}) async-start(f32[16,16,1280]{2,1,0:T(8,128)} %broadcast_in_dim.32), calls=%async_computation.1 | async-start | bytes 2621440 | tf_op jit(solution)/shard_map/all_to_all | solution.py:21
  128.1 140.4 %all-gather.15.cloned.1.call-start = ((), (), s32[]{:S(2)}) async-start(), calls=%async_computation.7 | async-start | bytes 4456448 | tf_op jit(solution)/shard_map/all_gather | solution.py:29
  131.1 1.7 copy-start.11
  131.1 1.7 copy-start.28
  169.8 46.4 %copy-start.14 = (f32[256,256]{1,0:T(8,128)}, f32[256,256]{1,0:T(8,128)S(1)}, u32[]{:S(2)}) copy-start(f32[256,256]{1,0:T(8,128)S(1)} %reduce_sum.280) | copy-start | bytes 786436
  216.3 3.9 copy-start.22
  220.2 55.6 %copy-start.1 = (f32[16,16,1280]{2,1,0:T(8,128)}, f32[16,16,1280]{2,1,0:T(8,128)S(1)}, u32[]{:S(2)}) copy-start(f32[16,16,1280]{2,1,0:T(8,128)S(1)} %get-tuple-element.15) | copy-start | bytes 3932164
  223.9 38.3 %all-to-all-start.2 = ((f32[16,16,1280]{2,1,0:T(8,128)}), f32[16,16,1280]{2,1,0:T(8,128)}, u32[]{:S(2)}, u32[]{:S(2)}) async-start(f32[16,16,1280]{2,1,0:T(8,128)} %broadcast_in_dim.33), calls=%async_computation.2 | async-start | bytes 2621440 | tf_op jit(solution)/shard_map/all_to_all | solution.py:21
  230.5 150.5 %all-gather.17.cloned.1.call-start = ((), (), s32[]{:S(2)}) async-start(), calls=%async_computation.8 | async-start | bytes 4456448 | tf_op jit(solution)/shard_map/all_gather | solution.py:29
  234.8 1.7 copy-start.7
  234.8 1.8 copy-start.12
  234.8 1.8 copy-start.29
  326.5 5.3 copy-start.23
  331.9 1.7 copy-start.17
  334.8 38.5 %all-to-all-start.3 = ((f32[16,16,1280]{2,1,0:T(8,128)}), f32[16,16,1280]{2,1,0:T(8,128)}, u32[]{:S(2)}, u32[]{:S(2)}) async-start(f32[16,16,1280]{2,1,0:T(8,128)} %broadcast_in_dim.34), calls=%async_computation.3 | async-start | bytes 2621440 | tf_op jit(solution)/shard_map/all_to_all | solution.py:21
  341.5 147.9 %all-gather.19.cloned.1.call-start = ((), (), s32[]{:S(2)}) async-start(), calls=%async_computation.9 | async-start | bytes 4456448 | tf_op jit(solution)/shard_map/all_gather | solution.py:29
  345.2 1.1 copy-start.8
  345.2 1.1 copy-start.30
  351.5 24.7 %copy-start.2 = (f32[16,16,1280]{2,1,0:T(8,128)S(1)}, f32[16,16,1280]{2,1,0:T(8,128)}, u32[]{:S(2)}) copy-start(f32[16,16,1280]{2,1,0:T(8,128)} %get-tuple-element.12) | copy-start | bytes 3932164
  437.0 4.9 copy-start.24
  440.8 1.1 copy-start.4
  440.8 2.7 copy-start.18
  444.8 6.1 %copy-start.5 = (f32[16,16,1280]{2,1,0:T(8,128)S(1)}, f32[16,16,1280]{2,1,0:T(8,128)}, u32[]{:S(2)}) copy-start(f32[16,16,1280]{2,1,0:T(8,128)} %copy-done.4) | copy-start | bytes 3932164
  444.8 37.8 %all-to-all-start.4 = ((f32[16,16,1280]{2,1,0:T(8,128)}), f32[16,16,1280]{2,1,0:T(8,128)}, u32[]{:S(2)}, u32[]{:S(2)}) async-start(f32[16,16,1280]{2,1,0:T(8,128)} %broadcast_in_dim.35), calls=%async_computation.4 | async-start | bytes 2621440 | tf_op jit(solution)/shard_map/all_to_all | solution.py:21
  454.1 1.1 copy-start.9
  454.1 1.1 copy-start.31
  492.6 4.3 copy-start.3
Sparse Core Ops, SparseCore 0:
  10.4 54.5 all-gather.10
  120.7 46.2 all-gather.12
  222.0 46.5 all-gather.14
  333.7 46.9 all-gather.16
  443.7 45.7 all-gather.18
where the time goes:
time: 573 us; the launch traced here: 564 us
  blocking collectives  211 us (37%)
  waiting for transfers between devices  125 us (22%)
  other arithmetic  71.2 us (12%)
  local copies, waits for them, and re-layouts  47.4 us (8%)
  starting transfers between devices  38.5 us (7%)
  matrix products  36.9 us (6%)
  between operations  33.8 us (6%)
    psum x25, blocking collectives, by_axis(): value = lax.psum(value, axis)  211 us
    all_to_all x5, waiting for transfers between devices, copy_for_each(): return lax.all_to_all(copies, axis, split_axis=0, concat_axis=0, tiled=True)  111 us
    all_to_all x5, starting transfers between devices, copy_for_each(): return lax.all_to_all(copies, axis, split_axis=0, concat_axis=0, tiled=True)  37.4 us
    dot_general x5, matrix products, local(): jnp.dot(prices.reshape(row_count, zone_count), onehot.T, precision=lax.Pr...  22.2 us
    reduce_sum x5, other arithmetic, local(): gap_local = jnp.sum(dispatch * low_dual + (capacity - dispatch) * high_dual)  16.9 us
    reduce_sum x5, other arithmetic, over_pieces(): return blocks.sum(axis=0)  14.5 us
    all_gather x5, waiting for transfers between devices, over_pieces(): blocks = lax.all_gather(value, axis)  13.8 us
    reshape x5, local copies, waits for them, and re-layouts, local(): (own_part + cross_part * block_mask[None, :, None]).reshape(local_scen, p...  12 us
  transfers between devices with their start and end apart: 10, of which 8 were waited for; matrix products, arithmetic and copies ran while one was open for 13% of the time, Pallas kernels for 0%

commit v1 on v0

v1 whole, which is shorter than its diff:
```python
import functools
import itertools

import jax
import jax.numpy as jnp
from jax import lax
from jax.experimental import pallas as pl
from jax.experimental.pallas import tpu as pltpu
from jax.sharding import PartitionSpec as P

ITERS = 5
MESH = pl.DeviceIdType.MESH
F32 = jnp.float32
BF16 = jnp.bfloat16
LANES = 128

penalty = 2.0
centering = 0.5
epsilon = 1e-06


def ring_hops(offset, size):
    return min(offset, size - offset)


def partners(dims, weights):
    result = []
    for offset in itertools.product(*[range(n) for n in dims]):
        if not any(offset):
            continue
        hops = sum(w * ring_hops(o, n) for o, n, w in zip(offset, dims, weights))
        back = 0
        for o, n in zip(offset, dims):
            back = back * n + (n - o) % n
        result.append((hops, offset, back - 1))
    result.sort(key=lambda item: -item[0])
    return [(offset, slot) for _, offset, slot in result]


def member(me, dims, offset):
    index = 0
    stride = 1
    for n, o in zip(reversed(dims), reversed(offset)):
        coordinate = (me // stride) % n
        index = index + ((coordinate + o) % n) * stride
        stride *= n
    return index


def kernel(
    scen_dims,
    gen_dims,
    entries,
    zone_entries,
    zone_scale,
    load_ref,
    linear_ref,
    diag_ref,
    cap_ref,
    cost_ref,
    coupling_ref,
    map_ref,
    zone_ref,
    numer_ref,
    denom_ref,
    x_ref,
    prices_ref,
    plan_ref,
    low_ref,
    high_ref,
    res_ref,
    inv_ref,
    onehot_ref,
    masked_ref,
    xb_ref,
    zp_ref,
    zr_ref,
    cs_ref,
    cr_ref,
    ts_ref,
    tr_ref,
    pg_ref,
    imb_ref,
    us_ref,
    ur_ref,
    send_sem,
    recv_sem,
):
    me_s = lax.axis_index("scen")
    me_g = lax.axis_index("gen")
    n_s = 1
    for n in scen_dims:
        n_s *= n
    n_g = 1
    for n in gen_dims:
        n_g *= n
    scen_partners = [
        (member(me_s, scen_dims, offset), slot)
        for offset, slot in partners(scen_dims, (1,) + (2,) * (len(scen_dims) - 1))
    ]
    gen_partners = [
        (member(me_g, gen_dims, offset), slot)
        for offset, slot in partners(gen_dims, (2,) * (len(gen_dims) - 1) + (1,))
    ]

    barrier = pltpu.get_barrier_semaphore()
    for target, _ in scen_partners:
        pl.semaphore_signal(barrier, inc=1, device_id={"scen": target}, device_id_type=MESH)
    for target, _ in gen_partners:
        pl.semaphore_signal(barrier, inc=1, device_id={"gen": target}, device_id_type=MESH)

    rows, width = x_ref.shape
    periods = linear_ref.shape[0]
    scens = rows // periods
    zones = zp_ref.shape[1]
    blocks, tile, _ = cost_ref.shape
    tiles = tile // LANES
    lane_tiles = width // LANES
    halves = periods // 8
    group = cs_ref.shape[0] // periods
    share = rows // n_g
    plan_rows = pg_ref.shape[0] // n_s
    total_scen = scens * n_s

    def columns(j):
        return pl.ds(j * tile, tile)

    def scen_rows(s):
        return pl.ds(pl.multiple_of(s * periods, periods), periods)

    for j in range(blocks):
        zone_row = zone_ref[:, columns(j)]
        ids = lax.broadcasted_iota(jnp.int32, (zones, tile), 0)
        onehot_ref[:, columns(j)] = jnp.where(ids == zone_row, 1.0, 0.0).astype(BF16)
        mask = map_ref[0, j].astype(F32)
        masked_ref[j] = (coupling_ref[j].astype(F32) * mask).astype(BF16)

    def begin(s, carry):
        ids = jnp.full((periods, width), me_s * scens + s, jnp.int32)
        level = 0.2 + 0.6 * (ids.astype(F32) + 0.5) / total_scen
        x_ref[scen_rows(s), :] = level * cap_ref[...]
        low_ref[scen_rows(s), :] = jnp.ones((periods, width), F32)
        high_ref[scen_rows(s), :] = jnp.ones((periods, width), F32)
        return carry

    lax.fori_loop(0, scens, begin, 0)
    prices_ref[...] = jnp.zeros_like(prices_ref)
    cs_ref[...] = jnp.zeros_like(cs_ref)
    ts_ref[...] = jnp.zeros_like(ts_ref)
    us_ref[...] = jnp.zeros_like(us_ref)
    pg_ref[...] = jnp.zeros_like(pg_ref)

    pl.semaphore_wait(barrier, len(scen_partners) + len(gen_partners))

    def scen_send(kind, source, landing):
        for target, slot in scen_partners:
            pltpu.make_async_remote_copy(
                src_ref=source(target),
                dst_ref=landing(slot),
                send_sem=send_sem.at[kind],
                recv_sem=recv_sem.at[kind],
                device_id={"scen": target},
                device_id_type=MESH,
            ).start()

    def gen_send(kind, source, landing):
        for target, slot in gen_partners:
            pltpu.make_async_remote_copy(
                src_ref=source(target),
                dst_ref=landing(slot),
                send_sem=send_sem.at[kind],
                recv_sem=recv_sem.at[kind],
                device_id={"gen": target},
                device_id_type=MESH,
            ).start()

    def wait_for(sem, span):
        pltpu.make_async_copy(span, span, sem).wait()

    ZONE, COLUMN, TERM, PLAN, IMB, ALL = range(6)
    spans = {
        ZONE: zr_ref,
        COLUMN: cr_ref,
        TERM: tr_ref,
        PLAN: pg_ref.at[pl.ds(0, (n_s - 1) * plan_rows)],
        IMB: imb_ref.at[pl.ds(0, (n_g - 1) * share)],
        ALL: ur_ref,
    }

    def iteration(k, carry):
        step = jnp.full((1, 1), numer_ref[k], jnp.int32).astype(F32) / jnp.full(
            (1, 1), denom_ref[k], jnp.int32
        ).astype(F32)

        for j in range(blocks):
            value = x_ref[:, columns(j)]
            high_part = value.astype(BF16)
            low_part = (value - high_part.astype(F32)).astype(BF16)
            xb_ref[:, columns(j)] = high_part
            onehot = onehot_ref[:, columns(j)]
            contract = (((1,), (1,)), ((), ()))
            found = lax.dot_general(
                high_part, onehot, contract, preferred_element_type=F32
            ) + lax.dot_general(low_part, onehot, contract, preferred_element_type=F32)
            if j == 0:
                zp_ref[...] = found
            else:
                zp_ref[...] += found
        gen_send(
            ZONE,
            lambda t: zp_ref.at[pl.ds(t * share, share)],
            lambda slot: zr_ref.at[pl.ds(slot * share, share)],
        )

        price = prices_ref[...]
        price_high = price.astype(BF16)
        price_low = (price - price_high.astype(F32)).astype(BF16)
        gap_row = jnp.zeros((1, LANES), F32)
        square_row = jnp.zeros((1, LANES), F32)
        for j in range(blocks):
            left = xb_ref[:, columns(j)]
            onehot = onehot_ref[:, columns(j)]
            res_ref[:, columns(j)] = (
                jnp.dot(left, cost_ref[j], preferred_element_type=F32)
                + jnp.dot(left, masked_ref[j], preferred_element_type=F32)
                + jnp.dot(price_high, onehot, preferred_element_type=F32)
                + jnp.dot(price_low, onehot, preferred_element_type=F32)
            )
            diag = diag_ref[:, columns(j)]
            cap = cap_ref[:, columns(j)]
            linear = linear_ref[:, columns(j)]

            def part(s, sums):
                column, rest, gap, square = sums
                here = (scen_rows(s), columns(j))
                value = x_ref[here]
                low = low_ref[here]
                high = high_ref[here]
                residual = res_ref[here] + (diag + penalty) * value + linear - low + high
                res_ref[here] = residual
                gap = gap + (value * low + (cap - value) * high)
                return column + value, rest + residual, gap, square + residual * residual

            zero = jnp.zeros((periods, tile), F32)
            column, rest, gap, square = lax.fori_loop(
                0, scens, part, (zero, zero, zero, zero), unroll=2
            )
            for t in range(tiles):
                lanes = slice(t * LANES, (t + 1) * LANES)
                gap_row = gap_row + jnp.sum(gap[:, lanes], axis=0, keepdims=True)
                square_row = square_row + jnp.sum(square[:, lanes], axis=0, keepdims=True)
                for h in range(halves):
                    first = h * 8 * group + j * tiles + t
                    cs_ref[pl.ds(first, 8, stride=group), :] = column[h * 8 : h * 8 + 8, lanes]
                    cs_ref[pl.ds(first + lane_tiles, 8, stride=group), :] = rest[
                        h * 8 : h * 8 + 8, lanes
                    ]
        for h in range(halves):
            first = h * 8 * group + 2 * lane_tiles
            cs_ref[pl.ds(first, 8, stride=group), :] = jnp.broadcast_to(gap_row, (8, LANES))
            cs_ref[pl.ds(first + 1, 8, stride=group), :] = jnp.broadcast_to(square_row, (8, LANES))
        scen_send(
            COLUMN,
            lambda t: cs_ref.at[pl.ds(t * group, group)],
            lambda slot: cr_ref.at[pl.ds(slot * group, group)],
        )

        mine = pl.ds(pl.multiple_of(me_g * share, share), share)
        wait_for(recv_sem.at[ZONE], spans[ZONE])
        total = zp_ref[mine, :]
        for slot in range(n_g - 1):
            total = total + zr_ref[slot * share : (slot + 1) * share, :]
        imbalance = total * zone_scale - load_ref[mine, :]
        imb_ref[mine, :] = imbalance
        primal = jnp.sum(imbalance * imbalance, axis=0, keepdims=True)
        primal_row = jnp.zeros((1, LANES), F32)
        for t in range(zones // LANES):
            primal_row = primal_row + primal[:, t * LANES : (t + 1) * LANES]
        gen_send(
            IMB,
            lambda t: imb_ref.at[mine],
            lambda slot: imb_ref.at[mine],
        )

        wait_for(recv_sem.at[COLUMN], spans[COLUMN])
        sums = cs_ref[pl.ds(pl.multiple_of(me_s * group, 8), group), :]
        for slot in range(n_s - 1):
            sums = sums + cr_ref[slot * group : (slot + 1) * group, :]
        plan = sums[:lane_tiles] / total_scen
        rest = sums[lane_tiles : 2 * lane_tiles]
        term = (2.0 * penalty) * plan * ((penalty / 2.0) * total_scen * plan - rest)
        term_row = jnp.sum(term, axis=0, keepdims=True)
        gap_row = sums[2 * lane_tiles : 2 * lane_tiles + 1]
        square_row = sums[2 * lane_tiles + 1 : 2 * lane_tiles + 2]
        own = pl.multiple_of(me_s * plan_rows, plan_rows)
        ts_ref[0:1, :] = term_row
        ts_ref[1:2, :] = primal_row
        scen_send(
            TERM,
            lambda t: ts_ref,
            lambda slot: tr_ref.at[pl.ds(slot * 8, 8)],
        )
        pg_ref[pl.ds(own, lane_tiles), :] = plan
        scen_send(
            PLAN,
            lambda t: pg_ref.at[pl.ds(own, plan_rows)],
            lambda slot: pg_ref.at[pl.ds(own, plan_rows)],
        )

        for j in range(blocks):
            diag = diag_ref[:, columns(j)]
            cap = cap_ref[:, columns(j)]

            def scale(s, none):
                here = (scen_rows(s), columns(j))
                value = x_ref[here]
                scaling = (
                    diag + penalty + low_ref[here] / value + high_ref[here] / (cap - value)
                )
                inv_ref[here] = step / scaling
                return none

            lax.fori_loop(0, scens, scale, 0, unroll=2)

        wait_for(recv_sem.at[TERM], spans[TERM])
        both = ts_ref[...]
        for slot in range(n_s - 1):
            both = both + tr_ref[slot * 8 : (slot + 1) * 8, :]
        us_ref[0:1, :] = both[0:1] + square_row
        us_ref[1:2, :] = both[1:2]
        us_ref[2:3, :] = gap_row
        gen_send(
            ALL,
            lambda t: us_ref,
            lambda slot: ur_ref.at[pl.ds(slot * 8, 8)],
        )
        wait_for(recv_sem.at[PLAN], spans[PLAN])
        for j in range(blocks):
            pieces = [
                jnp.concatenate(
                    [
                        pg_ref[
                            pl.ds(h * 8 * plan_rows + j * tiles + t, 8, stride=plan_rows), :
                        ]
                        for t in range(tiles)
                    ],
                    axis=1,
                )
                for h in range(halves)
            ]
            plan_ref[:, columns(j)] = jnp.concatenate(pieces, axis=0)
        wait_for(recv_sem.at[IMB], spans[IMB])
        wait_for(recv_sem.at[ALL], spans[ALL])
        every = us_ref[...]
        for slot in range(n_g - 1):
            every = every + ur_ref[slot * 8 : (slot + 1) * 8, :]
        every = jnp.sum(every, axis=1, keepdims=True)
        dual_rms = jnp.sqrt(every[0:1] / entries + epsilon)
        primal_rms = jnp.sqrt(every[1:2] / zone_entries + epsilon)
        target = centering * every[2:3] / (2.0 * entries)
        shrink = 1.0 / (1.0 + dual_rms)
        prices_ref[...] += (step / (1.0 + primal_rms)) * imb_ref[...]

        for j in range(blocks):
            cap = cap_ref[:, columns(j)]
            lowest = 0.02 * cap
            highest = 0.98 * cap
            twice = penalty * plan_ref[:, columns(j)]

            def update(s, none):
                here = (scen_rows(s), columns(j))
                low = low_ref[here]
                high = high_ref[here]
                move = (res_ref[here] - twice) * inv_ref[here] * shrink
                value = jnp.clip(x_ref[here] - move, lowest, highest)
                x_ref[here] = value
                low_ref[here] = low + step * (target / value - low)
                high_ref[here] = high + step * (target / (cap - value) - high)
                return none

            lax.fori_loop(0, scens, update, 0, unroll=2)

        for kind, span in spans.items():
            wait_for(send_sem.at[kind], span)
        return carry

    lax.fori_loop(0, ITERS, iteration, 0)


def solution(mesh):
    n_s, n_g = mesh.shape["scen"], mesh.shape["gen"]
    scen_dims = (n_s // 2, 2)
    gen_dims = (2, n_g // 4, 2) if n_g >= 4 else (n_g,)

    def local(
        zone_load,
        linear_cost,
        cost_diag,
        capacity,
        cost_tiles,
        coupling_tiles,
        block_map,
        zone_index,
        step_numer,
        step_denom,
    ):
        scens, periods, zones = zone_load.shape
        width = capacity.shape[0]
        blocks, tile, _ = cost_tiles.shape
        rows = scens * periods
        lane_tiles = width // LANES
        group = -(-(2 * lane_tiles + 2) // 8) * 8
        plan_rows = -(-lane_tiles // 8) * 8
        entries = float(n_s * rows * width * n_g)
        zone_entries = float(n_s * rows * zones)
        vmem = pl.BlockSpec(memory_space=pltpu.VMEM)
        smem = pl.BlockSpec(memory_space=pltpu.SMEM)
        state = pltpu.VMEM((rows, width), F32)
        share = rows // n_g
        dispatch, prices, plan = pl.pallas_call(
            functools.partial(
                kernel,
                scen_dims,
                gen_dims,
                entries,
                zone_entries,
                zones / (width * n_g),
            ),
            out_shape=(
                jax.ShapeDtypeStruct((rows, width), F32),
                jax.ShapeDtypeStruct((rows, zones), F32),
                jax.ShapeDtypeStruct((periods, width), F32),
            ),
            in_specs=[vmem] * 6 + [smem, vmem, smem, smem],
            out_specs=(vmem, vmem, vmem),
            scratch_shapes=[
                state,
                state,
                state,
                state,
                pltpu.VMEM((zones, width), BF16),
                pltpu.VMEM((blocks, tile, tile), BF16),
                pltpu.VMEM((rows, width), BF16),
                pltpu.VMEM((rows, zones), F32),
                pltpu.VMEM(((n_g - 1) * share, zones), F32),
                pltpu.VMEM((periods * group, LANES), F32),
                pltpu.VMEM(((n_s - 1) * group, LANES), F32),
                pltpu.VMEM((8, LANES), F32),
                pltpu.VMEM(((n_s - 1) * 8, LANES), F32),
                pltpu.VMEM((n_s * plan_rows, LANES), F32),
                pltpu.VMEM((rows, zones), F32),
                pltpu.VMEM((8, LANES), F32),
                pltpu.VMEM(((n_g - 1) * 8, LANES), F32),
                pltpu.SemaphoreType.DMA((6,)),
                pltpu.SemaphoreType.DMA((6,)),
            ],
            compiler_params=pltpu.CompilerParams(collective_id=0, has_side_effects=True),
        )(
            zone_load.reshape(rows, zones),
            linear_cost,
            cost_diag.reshape(1, width),
            capacity.reshape(1, width),
            cost_tiles,
            coupling_tiles[0],
            block_map,
            zone_index.reshape(1, width),
            step_numer,
            step_denom,
        )
        return dispatch.reshape(scens, periods, width), prices.reshape(scens, periods, zones), plan

    return jax.shard_map(
        local,
        mesh=mesh,
        in_specs=(
            P("scen", None, None),
            P(None, "gen"),
            P("gen"),
            P("gen"),
            P("gen", None, None),
            P("scen", "gen", None, None),
            P("scen", "gen"),
            P("gen"),
            P(),
            P(),
        ),
        out_specs=(P("scen", None, "gen"), P("scen", None, None), P(None, "gen")),
        check_vma=False,
    )
```

time: 573 us -> 136 us (0.24); the launches traced: 564 us -> 136 us
  blocking collectives: 211 us -> 0 us
  Pallas kernels: 0 us -> 127 us
  waiting for transfers between devices: 125 us -> 0 us
  other arithmetic: 71.2 us -> 0 us
  local copies, waits for them, and re-layouts: 47.4 us -> 7.74 us
  starting transfers between devices: 38.5 us -> 0 us
  matrix products: 36.9 us -> 0 us
  between operations: 33.8 us -> 0.66 us
    psum x25 -> x0, blocking collectives: 211 us -> none  [by_axis(): value = lax.psum(value, axis)]
    pallas_call x0 -> x1, Pallas kernels: none -> 127 us  [local(): pl.pallas_call(functools.partial(kernel, scen_dims, gen_dims, entries, zo...]
    all_to_all x5 -> x0, waiting for transfers between devices: 111 us -> none  [copy_for_each(): return lax.all_to_all(copies, axis, split_axis=0, concat_axis=0, tiled=True)]
    reduce_sum x20 -> x0, other arithmetic: 45 us -> none  [the longest x5 16.9 us: local(): gap_local = jnp.sum(dispatch * low_dual + (capacity - dispatch) * high_dual)]
    all_to_all x5 -> x0, starting transfers between devices: 37.4 us -> none  [copy_for_each(): return lax.all_to_all(copies, axis, split_axis=0, concat_axis=0, tiled=True)]
    dot_general x20 -> x0, matrix products: 36.9 us -> none  [the longest x5 22.2 us: local(): jnp.dot(prices.reshape(row_count, zone_count), onehot.T, precision=lax.Pr...]
    reshape x10 -> x3, local copies, waits for them, and re-layouts: 20.5 us -> 3.88 us  [the longest x1 1.29 us: local(): cost_diag.reshape(1, width)]
    all_gather x5 -> x0, waiting for transfers between devices: 13.8 us -> none  [over_pieces(): blocks = lax.all_gather(value, axis)]
  transfers between devices with their start and end apart: 10 -> 0, of which waited for: 8 -> 0; matrix products, arithmetic and copies ran while one was open for 13% -> 0% of each run, Pallas kernels for 0% -> 0%
where the time goes in v1:
time: 136 us
  Pallas kernels  127 us (93%)
  local copies, waits for them, and re-layouts  7.74 us (6%)
    pallas_call x1, Pallas kernels, local(): pl.pallas_call(functools.partial(kernel, scen_dims, gen_dims, entries, zo...  127 us
    unnamed x7, local copies, waits for them, and re-layouts  3.86 us

profile of v1, /device:TPU:1, one launch (start us, length us, event | category | flops | bytes accessed | tf_op | source)
XLA Modules:
  0.0 135.5 jit_solution(18335455230990241056)
XLA Ops:
  0.6 1.3 reshape.25.diag_ref
  1.9 1.3 reshape.26.cap_ref
  3.2 1.3 reshape.27.zone_ref
  4.5 127.1 %shard_map.121 = (f32[256,1280]{1,0:T(8,128)}, f32[256,256]{1,0:T(8,128)}, f32[16,1280]{1,0:T(8,128)}) custom-call(f32[256,256]{1,0:T(8,128)} %bitcast.7, f32[16,1280]{1,0:T(8,128)} %linear_ref.1, f32[1,1280]{1,0:T(1,128)} %reshape.25.diag_ref, f32[1,1280]{1,0:T(1,128)} %reshape.26.cap_ref, bf16[5,256,256]{2,1,0:T(8,128)(2,1)} %cost_ref.1, ...), custom_call_target="tpu_custom_call" | custom-call | tf_op jit(solution)/shard_map/pallas_call | solution.py:420
  131.6 0.0 copy-start
  131.6 0.0 copy-start.1
  131.6 2.5 %copy.16 = f32[16,16,1280]{2,1,0:T(8,128)} copy(f32[16,16,1280]{2,1,0:T(8,128)} %bitcast.4) | data formatting | bytes 2621440
  134.2 0.0 copy-done
  134.2 0.7 copy.17
  134.9 0.0 copy-done.1
  134.9 0.6 copy.18
Async XLA Ops:
  131.6 2.5 %copy-start = (f32[256,256]{1,0:T(8,128)S(1)}, f32[256,256]{1,0:T(8,128)}, u32[]{:S(2)}) copy-start(f32[256,256]{1,0:T(8,128)} %get-tuple-element.7) | copy-start | bytes 786436
  131.6 3.2 %copy-start.1 = (f32[16,1280]{1,0:T(8,128)S(1)}, f32[16,1280]{1,0:T(8,128)}, u32[]{:S(2)}) copy-start(f32[16,1280]{1,0:T(8,128)} %get-tuple-element.14) | copy-start | bytes 245764

commit v2 on v1

v2 whole, which is shorter than its diff:
```python
import functools
import itertools

import jax
import jax.numpy as jnp
from jax import lax
from jax.experimental import pallas as pl
from jax.experimental.pallas import tpu as pltpu
from jax.sharding import PartitionSpec as P

ITERS = 5
MESH = pl.DeviceIdType.MESH
F32 = jnp.float32
BF16 = jnp.bfloat16
LANES = 128

penalty = 2.0
centering = 0.5
epsilon = 1e-06


def ring(offset, size):
    return min(offset, size - offset)


def partners(dims, hops):
    result = []
    for offset in itertools.product(*[range(n) for n in dims]):
        if not any(offset):
            continue
        back = 0
        for o, n in zip(offset, dims):
            back = back * n + (n - o) % n
        result.append((hops(offset), offset, back - 1))
    result.sort(key=lambda item: -item[0])
    return [(offset, slot) for _, offset, slot in result]


def moved(me, dims, offset):
    index = 0
    stride = 1
    for n, o in zip(reversed(dims), reversed(offset)):
        coordinate = (me // stride) % n
        index = index + ((coordinate + o) % n) * stride
        stride *= n
    return index


def two_parts(value):
    high = value.astype(BF16)
    return high, (value - high.astype(F32)).astype(BF16)


def kernel(
    scen_dims,
    gen_dims,
    entries,
    zone_entries,
    zone_scale,
    load_ref,
    linear_ref,
    diag_in,
    cap_in,
    cost_ref,
    coupling_ref,
    map_ref,
    zone_in,
    numer_ref,
    denom_ref,
    x_ref,
    prices_ref,
    plan_ref,
    low_ref,
    high_ref,
    res_ref,
    inv_ref,
    onehot_ref,
    turned_ref,
    masked_ref,
    diag_ref,
    cap_ref,
    column_ref,
    round_ref,
    dual_ref,
    paid_ref,
    more_ref,
    zc_ref,
    zp_ref,
    zr_ref,
    cs_ref,
    cr_ref,
    pg_ref,
    imb_ref,
    ns_ref,
    nr_ref,
    fs_ref,
    fr_ref,
    all_ref,
    send_sem,
    recv_sem,
    far_sem,
):
    me_s = lax.axis_index("scen")
    me_g = lax.axis_index("gen")
    depth, sides = scen_dims
    n_s = depth * sides
    n_g = gen_dims[0] * gen_dims[1] * gen_dims[2]
    y_hops = {(0, 0): 0, (0, 1): 1, (1, 0): 2, (1, 1): 1}

    def scen_device(offset):
        return {"scen": moved(me_s, scen_dims, offset)}

    def gen_device(offset):
        return {"gen": moved(me_g, gen_dims, offset)}

    def plane_device(offset):
        return {
            "scen": moved(me_s, scen_dims, (0, offset[0])),
            "gen": moved(me_g, gen_dims, offset[1:]),
        }

    scen_group = partners(scen_dims, lambda o: ring(o[0], depth) + 2 * o[1])
    gen_group = partners(gen_dims, lambda o: 2 * o[0] + 2 * ring(o[1], gen_dims[1]) + o[2])
    line_group = partners((depth,), lambda o: ring(o[0], depth))
    plane_group = partners(
        (sides,) + gen_dims,
        lambda o: 2 * y_hops[o[:2]] + 2 * ring(o[2], gen_dims[1]) + o[3],
    )
    scen_to = [(scen_device(o), moved(me_s, scen_dims, o), slot) for o, slot in scen_group]
    gen_to = [(gen_device(o), moved(me_g, gen_dims, o), slot) for o, slot in gen_group]
    line_to = [(scen_device((o[0], 0)), 0, slot) for o, slot in line_group]
    plane_to = [(plane_device(o), 0, slot) for o, slot in plane_group]

    barrier = pltpu.get_barrier_semaphore()
    greeted = [device for device, _, _ in scen_to]
    greeted += [plane_device(o) for o, _ in plane_group if any(o[1:])]
    for device in greeted:
        pl.semaphore_signal(barrier, inc=1, device_id=device, device_id_type=MESH)

    rows, width = x_ref.shape
    periods = linear_ref.shape[0]
    scens = rows // periods
    zones = zp_ref.shape[1]
    blocks, tile, _ = cost_ref.shape
    tiles = tile // LANES
    lane_tiles = width // LANES
    halves = periods // 8
    group = cs_ref.shape[0] // periods
    share = rows // n_g
    plan_rows = pg_ref.shape[0] // n_s
    total_scen = scens * n_s
    mine = pl.ds(pl.multiple_of(me_g * share, share), share)
    own = pl.multiple_of(me_s * plan_rows, plan_rows)

    def columns(j):
        return pl.ds(j * tile, tile)

    def scen_rows(s):
        return pl.ds(pl.multiple_of(s * periods, periods), periods)

    def send(kind, to, source, landing, sem=None):
        for device, member, slot in to:
            pltpu.make_async_remote_copy(
                src_ref=source(member),
                dst_ref=landing(slot),
                send_sem=send_sem.at[kind],
                recv_sem=recv_sem.at[kind] if sem is None else sem,
                device_id=device,
                device_id_type=MESH,
            ).start()

    def wait_for(sem, span):
        pltpu.make_async_copy(span, span, sem).wait()

    ZONE, COLUMN, PLAN, IMB, NEAR, FAR, START = range(7)
    spans = {
        ZONE: zr_ref,
        COLUMN: cr_ref,
        PLAN: pg_ref.at[pl.ds(0, (n_s - 1) * plan_rows)],
        IMB: imb_ref.at[pl.ds(0, (n_g - 1) * share)],
        NEAR: nr_ref,
        FAR: fr_ref.at[0],
        START: zc_ref.at[pl.ds(0, n_g - 1)],
    }

    def level(s, shape):
        ids = jnp.full(shape, me_s * scens + s, jnp.int32)
        return 0.2 + 0.6 * (ids.astype(F32) + 0.5) / total_scen

    def step_of(k):
        numer = jnp.full((1, 1), numer_ref[k], jnp.int32).astype(F32)
        return numer / jnp.full((1, 1), denom_ref[k], jnp.int32).astype(F32)

    def fold(value):
        row = jnp.sum(value, axis=0, keepdims=True)
        return sum(row[:, t * LANES : (t + 1) * LANES] for t in range(value.shape[1] // LANES))

    diag_ref[...] = diag_in[...].reshape(1, width)
    cap_ref[...] = cap_in[...].reshape(1, width)
    zone_row = zone_in[...].reshape(1, width)
    start = jnp.zeros((16, zones), F32)
    for j in range(blocks):
        ids = lax.broadcasted_iota(jnp.int32, (zones, tile), 0)
        onehot = jnp.where(ids == zone_row[:, j * tile : (j + 1) * tile], 1.0, 0.0)
        onehot_ref[:, columns(j)] = onehot.astype(BF16)
        turned = onehot.T.astype(BF16)
        turned_ref[columns(j), :] = turned
        cap_high, cap_low = two_parts(jnp.broadcast_to(cap_ref[:, columns(j)], (8, tile)))
        both = jnp.concatenate([cap_high, cap_low], axis=0)
        start = start + jnp.dot(both, turned, preferred_element_type=F32)
    zc_ref[me_g] = start[0:1] + start[8:9]

    pl.semaphore_wait(barrier, len(greeted))
    send(START, gen_to, lambda t: zc_ref.at[me_g], lambda slot: zc_ref.at[me_g])

    for j in range(blocks):
        mask = map_ref[0, j].astype(F32)
        masked_ref[j] = (coupling_ref[j].astype(F32) * mask).astype(BF16)

    def begin(s, carry):
        here = scen_rows(s)
        x_ref[here, :] = level(s, (periods, width)) * cap_ref[...]
        low_ref[here, :] = jnp.ones((periods, width), F32)
        high_ref[here, :] = jnp.ones((periods, width), F32)
        return carry

    lax.fori_loop(0, scens, begin, 0, unroll=2)
    prices_ref[...] = jnp.zeros_like(prices_ref)
    paid_ref[...] = jnp.zeros_like(paid_ref)
    cs_ref[...] = jnp.zeros_like(cs_ref)
    ns_ref[...] = jnp.zeros_like(ns_ref)
    pg_ref[...] = jnp.zeros_like(pg_ref)

    def residuals(step, first):
        if not first:
            price_high, price_low = two_parts(prices_ref[...])
        gap_row = jnp.zeros((1, LANES), F32)
        square_row = jnp.zeros((1, LANES), F32)
        keep = 1.0 - step
        for j in range(blocks):
            left = x_ref[:, columns(j)].astype(BF16)
            found = jnp.dot(left, cost_ref[j], preferred_element_type=F32) + jnp.dot(
                left, masked_ref[j], preferred_element_type=F32
            )
            if not first:
                onehot = onehot_ref[:, columns(j)]
                found = (
                    found
                    + jnp.dot(price_high, onehot, preferred_element_type=F32)
                    + jnp.dot(price_low, onehot, preferred_element_type=F32)
                )
            res_ref[:, columns(j)] = found
            cap = cap_ref[:, columns(j)]
            weight = diag_ref[:, columns(j)] + penalty
            fixed = linear_ref[:, columns(j)]
            if first:
                fixed = fixed - penalty * 0.5 * cap

            def part(s, sums):
                gap, square = sums
                here = (scen_rows(s), columns(j))
                value = x_ref[here]
                low = low_ref[here]
                high = high_ref[here]
                rest = cap - value
                residual = res_ref[here] + weight * value + fixed - low + high
                scale = step / (weight + low / value + high / rest)
                if first:
                    res_ref[here] = residual * scale
                else:
                    res_ref[here] = residual
                    inv_ref[here] = scale
                low_ref[here] = keep * low
                high_ref[here] = keep * high
                return gap + (value * low + rest * high), square + residual * residual

            zero = jnp.zeros((periods, tile), F32)
            gap, square = lax.fori_loop(0, scens, part, (zero, zero), unroll=2)
            gap_row = gap_row + fold(gap)
            square_row = square_row + fold(square)
        return gap_row, square_row

    def exchange(k, first):
        send(
            NEAR,
            line_to,
            lambda t: ns_ref,
            lambda slot: nr_ref.at[slot],
        )
        if not first:
            send(
                PLAN,
                scen_to,
                lambda t: pg_ref.at[pl.ds(own, plan_rows)],
                lambda slot: pg_ref.at[pl.ds(own, plan_rows)],
            )
        wait_for(recv_sem.at[NEAR], spans[NEAR])
        near = ns_ref[...]
        for slot in range(depth - 1):
            near = near + nr_ref[slot]
        fs_ref[...] = near
        turn = lax.rem(k, 2)
        send(
            FAR,
            plane_to,
            lambda t: fs_ref,
            lambda slot: fr_ref.at[turn, slot],
            far_sem.at[turn],
        )
        if not first:
            wait_for(recv_sem.at[IMB], spans[IMB])
        lumped = jnp.zeros((periods, zones), F32)
        for s in range(scens):
            lumped = lumped + imb_ref[s * periods : (s + 1) * periods, :]
        both = jnp.concatenate(two_parts(lumped), axis=0)
        for j in range(blocks):
            found = jnp.dot(both, onehot_ref[:, columns(j)], preferred_element_type=F32)
            more_ref[:, columns(j)] = found[:periods] + found[periods:]
        if not first:
            wait_for(recv_sem.at[PLAN], spans[PLAN])
            for j in range(blocks):
                pieces = [
                    jnp.concatenate(
                        [
                            pg_ref[
                                pl.ds(h * 8 * plan_rows + j * tiles + t, 8, stride=plan_rows), :
                            ]
                            for t in range(tiles)
                        ],
                        axis=1,
                    )
                    for h in range(halves)
                ]
                plan = jnp.concatenate(pieces, axis=0)
                plan_ref[:, columns(j)] = plan
                twice = penalty * plan

                def settle(s, none):
                    here = (scen_rows(s), columns(j))
                    res_ref[here] = (res_ref[here] - twice) * inv_ref[here]
                    return none

                lax.fori_loop(0, scens, settle, 0, unroll=4)
        wait_for(far_sem.at[turn], spans[FAR])
        every = fs_ref[...]
        for slot in range(n_g * sides - 1):
            every = every + fr_ref[turn, slot]
        all_ref[...] = jnp.broadcast_to(jnp.sum(every, axis=1, keepdims=True), (4, LANES))

    def scalars(step):
        every = all_ref[:, 0:1]
        dual_rms = jnp.sqrt(every[0:1] / entries + epsilon)
        primal_rms = jnp.sqrt(every[1:2] / zone_entries + epsilon)
        target = centering * every[2:3] / (2.0 * entries)
        return 1.0 / (1.0 + dual_rms), step / (1.0 + primal_rms), step * target

    step = step_of(0)
    gap_row, square_row = residuals(step, True)
    wait_for(recv_sem.at[START], spans[START])
    per_zone = jnp.sum(zc_ref[...], axis=0)

    def imbalances(s, none):
        here = scen_rows(s)
        imb_ref[here, :] = level(s, (periods, zones)) * per_zone * zone_scale - load_ref[here, :]
        return none

    lax.fori_loop(0, scens, imbalances, 0, unroll=2)
    imbalance = imb_ref[mine, :]
    ns_ref[0:1, :] = square_row
    ns_ref[1:2, :] = fold(imbalance * imbalance)
    ns_ref[2:3, :] = gap_row
    exchange(0, True)
    wait_for(send_sem.at[START], spans[START])
    for kind in (NEAR, FAR):
        wait_for(send_sem.at[kind], spans[kind])

    def iteration(k, carry):
        step = step_of(k)
        shrink, pay, pull = scalars(step)

        for j in range(blocks):
            cap = cap_ref[:, columns(j)]
            lowest = 0.02 * cap
            highest = 0.98 * cap

            def update(s, sums):
                column, rounded, dual = sums
                here = (scen_rows(s), columns(j))
                value = jnp.clip(x_ref[here] - res_ref[here] * shrink, lowest, highest)
                low = low_ref[here] + pull / value
                high = high_ref[here] + pull / (cap - value)
                x_ref[here] = value
                low_ref[here] = low
                high_ref[here] = high
                return (
                    column + value,
                    rounded + value.astype(BF16).astype(F32),
                    dual + (high - low),
                )

            zero = jnp.zeros((periods, tile), F32)
            column, rounded, dual = lax.fori_loop(
                0, scens, update, (zero, zero, zero), unroll=4
            )
            column_ref[:, columns(j)] = column
            round_ref[:, columns(j)] = rounded
            dual_ref[:, columns(j)] = dual

        for j in range(blocks):
            both = jnp.concatenate(two_parts(round_ref[:, columns(j)]), axis=0)
            found = jnp.dot(both, cost_ref[j], preferred_element_type=F32) + jnp.dot(
                both, masked_ref[j], preferred_element_type=F32
            )
            paid = paid_ref[:, columns(j)] + pay * more_ref[:, columns(j)]
            paid_ref[:, columns(j)] = paid
            column = column_ref[:, columns(j)]
            rest = (
                (found[:periods] + found[periods:])
                + (diag_ref[:, columns(j)] + penalty) * column
                + float(scens) * linear_ref[:, columns(j)]
                + paid
                + dual_ref[:, columns(j)]
            )
            for t in range(tiles):
                lanes = slice(t * LANES, (t + 1) * LANES)
                for h in range(halves):
                    first = h * 8 * group + j * tiles + t
                    cs_ref[pl.ds(first, 8, stride=group), :] = column[h * 8 : h * 8 + 8, lanes]
                    cs_ref[pl.ds(first + lane_tiles, 8, stride=group), :] = rest[
                        h * 8 : h * 8 + 8, lanes
                    ]
        send(
            COLUMN,
            scen_to,
            lambda t: cs_ref.at[pl.ds(t * group, group)],
            lambda slot: cr_ref.at[pl.ds(slot * group, group)],
        )
        prices_ref[...] += pay * imb_ref[...]

        found = None
        for j in range(blocks):
            for piece in two_parts(x_ref[:, columns(j)]):
                term = jnp.dot(piece, turned_ref[columns(j), :], preferred_element_type=F32)
                found = term if found is None else found + term
        zp_ref[...] = found
        send(
            ZONE,
            gen_to,
            lambda t: zp_ref.at[pl.ds(t * share, share)],
            lambda slot: zr_ref.at[pl.ds(slot * share, share)],
        )

        gap_row, square_row = residuals(step_of(k + 1), False)

        wait_for(recv_sem.at[ZONE], spans[ZONE])
        total = zp_ref[mine, :]
        for slot in range(n_g - 1):
            total = total + zr_ref[slot * share : (slot + 1) * share, :]
        imbalance = total * zone_scale - load_ref[mine, :]
        imb_ref[mine, :] = imbalance
        send(IMB, gen_to, lambda t: imb_ref.at[mine], lambda slot: imb_ref.at[mine])
        ns_ref[1:2, :] = fold(imbalance * imbalance)
        ns_ref[2:3, :] = gap_row

        wait_for(recv_sem.at[COLUMN], spans[COLUMN])
        sums = cs_ref[pl.ds(pl.multiple_of(me_s * group, 8), group), :]
        for slot in range(n_s - 1):
            sums = sums + cr_ref[slot * group : (slot + 1) * group, :]
        plan = sums[:lane_tiles] / total_scen
        rest = sums[lane_tiles : 2 * lane_tiles]
        term = (2.0 * penalty) * plan * ((penalty / 2.0) * total_scen * plan - rest)
        ns_ref[0:1, :] = square_row + jnp.sum(term, axis=0, keepdims=True)
        pg_ref[pl.ds(own, lane_tiles), :] = plan
        exchange(k + 1, False)
        for kind in (ZONE, COLUMN, PLAN, IMB, NEAR, FAR):
            wait_for(send_sem.at[kind], spans[kind])
        return carry

    lax.fori_loop(0, ITERS - 1, iteration, 0)

    shrink, pay, _ = scalars(step_of(ITERS - 1))
    prices_ref[...] += pay * imb_ref[...]
    for j in range(blocks):
        cap = cap_ref[:, columns(j)]
        lowest = 0.02 * cap
        highest = 0.98 * cap

        def finish(s, none):
            here = (scen_rows(s), columns(j))
            x_ref[here] = jnp.clip(x_ref[here] - res_ref[here] * shrink, lowest, highest)
            return none

        lax.fori_loop(0, scens, finish, 0, unroll=4)


def solution(mesh):
    n_s, n_g = mesh.shape["scen"], mesh.shape["gen"]
    scen_dims = (n_s // 2, 2)
    gen_dims = (2, n_g // 4, 2) if n_g >= 4 else (n_g, 1, 1)

    def local(
        zone_load,
        linear_cost,
        cost_diag,
        capacity,
        cost_tiles,
        coupling_tiles,
        block_map,
        zone_index,
        step_numer,
        step_denom,
    ):
        scens, periods, zones = zone_load.shape
        width = capacity.shape[0]
        blocks, tile, _ = cost_tiles.shape
        rows = scens * periods
        lane_tiles = width // LANES
        group = -(-(2 * lane_tiles) // 8) * 8
        plan_rows = -(-lane_tiles // 8) * 8
        entries = float(n_s * rows * width * n_g)
        zone_entries = float(n_s * rows * zones)
        vmem = pl.BlockSpec(memory_space=pltpu.VMEM)
        smem = pl.BlockSpec(memory_space=pltpu.SMEM)
        state = pltpu.VMEM((rows, width), F32)
        share = rows // n_g
        dispatch, prices, plan = pl.pallas_call(
            functools.partial(
                kernel,
                scen_dims,
                gen_dims,
                entries,
                zone_entries,
                zones / (width * n_g),
            ),
            out_shape=(
                jax.ShapeDtypeStruct((rows, width), F32),
                jax.ShapeDtypeStruct((rows, zones), F32),
                jax.ShapeDtypeStruct((periods, width), F32),
            ),
            in_specs=[vmem] * 6 + [smem, vmem, smem, smem],
            out_specs=(vmem, vmem, vmem),
            scratch_shapes=[
                state,
                state,
                state,
                state,
                pltpu.VMEM((zones, width), BF16),
                pltpu.VMEM((width, zones), BF16),
                pltpu.VMEM((blocks, tile, tile), BF16),
                pltpu.VMEM((1, width), F32),
                pltpu.VMEM((1, width), F32),
                pltpu.VMEM((periods, width), F32),
                pltpu.VMEM((periods, width), F32),
                pltpu.VMEM((periods, width), F32),
                pltpu.VMEM((periods, width), F32),
                pltpu.VMEM((periods, width), F32),
                pltpu.VMEM((n_g, 1, zones), F32),
                pltpu.VMEM((rows, zones), F32),
                pltpu.VMEM(((n_g - 1) * share, zones), F32),
                pltpu.VMEM((periods * group, LANES), F32),
                pltpu.VMEM(((n_s - 1) * group, LANES), F32),
                pltpu.VMEM((n_s * plan_rows, LANES), F32),
                pltpu.VMEM((rows, zones), F32),
                pltpu.VMEM((4, LANES), F32),
                pltpu.VMEM((scen_dims[0] - 1, 4, LANES), F32),
                pltpu.VMEM((4, LANES), F32),
                pltpu.VMEM((2, n_g * scen_dims[1] - 1, 4, LANES), F32),
                pltpu.VMEM((4, LANES), F32),
                pltpu.SemaphoreType.DMA((7,)),
                pltpu.SemaphoreType.DMA((7,)),
                pltpu.SemaphoreType.DMA((2,)),
            ],
            compiler_params=pltpu.CompilerParams(collective_id=0, has_side_effects=True),
        )(
            zone_load.reshape(rows, zones),
            linear_cost,
            cost_diag,
            capacity,
            cost_tiles,
            coupling_tiles[0],
            block_map,
            zone_index,
            step_numer,
            step_denom,
        )
        return dispatch.reshape(scens, periods, width), prices.reshape(scens, periods, zones), plan

    return jax.shard_map(
        local,
        mesh=mesh,
        in_specs=(
            P("scen", None, None),
            P(None, "gen"),
            P("gen"),
            P("gen"),
            P("gen", None, None),
            P("scen", "gen", None, None),
            P("scen", "gen"),
            P("gen"),
            P(),
            P(),
        ),
        out_specs=(P("scen", None, "gen"), P("scen", None, None), P(None, "gen")),
        check_vma=False,
    )
```

time: 136 us -> 107 us (0.79)
  Pallas kernels: 127 us -> 102 us
  local copies, waits for them, and re-layouts: 7.74 us -> 3.86 us
    pallas_call x1, Pallas kernels: 127 us -> 102 us  [local(): pl.pallas_call(functools.partial(kernel, scen_dims, gen_dims, entries, zo...]
    reshape x3 -> x0, local copies, waits for them, and re-layouts: 3.88 us -> none  [the longest x1 1.29 us: local(): cost_diag.reshape(1, width)]
where the time goes in v2:
time: 107 us
  Pallas kernels  102 us (95%)
  local copies, waits for them, and re-layouts  3.86 us (4%)
    pallas_call x1, Pallas kernels, local(): pl.pallas_call(functools.partial(kernel, scen_dims, gen_dims, entries, zo...  102 us
    unnamed x7, local copies, waits for them, and re-layouts  3.86 us

profile of v2, /device:TPU:1, one launch (start us, length us, event | category | flops | bytes accessed | tf_op | source)
XLA Modules:
  0.0 106.9 jit_solution(327619983131763617)
XLA Ops:
  0.6 102.4 %shard_map.121 = (f32[256,1280]{1,0:T(8,128)}, f32[256,256]{1,0:T(8,128)}, f32[16,1280]{1,0:T(8,128)}) custom-call(f32[256,256]{1,0:T(8,128)} %bitcast.7, f32[16,1280]{1,0:T(8,128)} %linear_ref.1, f32[1280]{0:T(1024)} %diag_in.1, f32[1280]{0:T(1024)} %cap_in.1, bf16[5,256,256]{2,1,0:T(8,128)(2,1)} %cost_ref.1, bf16[5,256,256]{2,1,0:T(8,128)(2,1)} %bitcast.5, ...), custom_call_target="tpu_custom_call" | custom-call | tf_op jit(solution)/shard_map/pallas_call | solution.py:526
  103.1 0.0 copy-start
  103.1 0.0 copy-start.1
  103.1 2.5 %copy.16 = f32[16,16,1280]{2,1,0:T(8,128)} copy(f32[16,16,1280]{2,1,0:T(8,128)} %bitcast.4) | data formatting | bytes 2621440
  105.6 0.0 copy-done
  105.6 0.7 copy.17
  106.3 0.0 copy-done.1
  106.3 0.6 copy.18
Async XLA Ops:
  103.1 2.5 %copy-start = (f32[256,256]{1,0:T(8,128)S(1)}, f32[256,256]{1,0:T(8,128)}, u32[]{:S(2)}) copy-start(f32[256,256]{1,0:T(8,128)} %get-tuple-element.7) | copy-start | bytes 786436
  103.1 3.2 %copy-start.1 = (f32[16,1280]{1,0:T(8,128)S(1)}, f32[16,1280]{1,0:T(8,128)}, u32[]{:S(2)}) copy-start(f32[16,1280]{1,0:T(8,128)} %get-tuple-element.14) | copy-start | bytes 245764

commit v3 on v2

--- a/solution.py
+++ b/solution.py
@@ -57,6 +57,19 @@
     entries,
     zone_entries,
     zone_scale,
+    load_hbm,
+    linear_hbm,
+    diag_hbm,
+    cap_hbm,
+    cost_hbm,
+    coupling_hbm,
+    map_hbm,
+    zone_hbm,
+    numer_hbm,
+    denom_hbm,
+    x_ref,
+    prices_ref,
+    plan_ref,
     load_ref,
     linear_ref,
     diag_in,
@@ -67,9 +80,6 @@
     zone_in,
     numer_ref,
     denom_ref,
-    x_ref,
-    prices_ref,
-    plan_ref,
     low_ref,
     high_ref,
     res_ref,
@@ -99,6 +109,7 @@
     send_sem,
     recv_sem,
     far_sem,
+    in_sem,
 ):
     me_s = lax.axis_index("scen")
     me_g = lax.axis_index("gen")
@@ -137,8 +148,26 @@
     for device in greeted:
         pl.semaphore_signal(barrier, inc=1, device_id=device, device_id_type=MESH)
 
+    fetched = {}
+    for position, (name, source, place) in enumerate(
+        (
+            ("zone", zone_hbm, zone_in),
+            ("cap", cap_hbm, cap_in),
+            ("diag", diag_hbm, diag_in),
+            ("cost", cost_hbm, cost_ref),
+            ("map", map_hbm, map_ref),
+            ("coupling", coupling_hbm, coupling_ref),
+            ("linear", linear_hbm, linear_ref),
+            ("numer", numer_hbm, numer_ref),
+            ("denom", denom_hbm, denom_ref),
+            ("load", load_hbm, load_ref),
+        )
+    ):
+        fetched[name] = pltpu.make_async_copy(source, place, in_sem.at[position])
+        fetched[name].start()
+
     rows, width = x_ref.shape
-    periods = linear_ref.shape[0]
+    periods = plan_ref.shape[0]
     scens = rows // periods
     zones = zp_ref.shape[1]
     blocks, tile, _ = cost_ref.shape
@@ -195,6 +224,8 @@
         row = jnp.sum(value, axis=0, keepdims=True)
         return sum(row[:, t * LANES : (t + 1) * LANES] for t in range(value.shape[1] // LANES))
 
+    for name in ("zone", "cap", "diag"):
+        fetched[name].wait()
     diag_ref[...] = diag_in[...].reshape(1, width)
     cap_ref[...] = cap_in[...].reshape(1, width)
     zone_row = zone_in[...].reshape(1, width)
@@ -213,6 +244,8 @@
     pl.semaphore_wait(barrier, len(greeted))
     send(START, gen_to, lambda t: zc_ref.at[me_g], lambda slot: zc_ref.at[me_g])
 
+    for name in ("map", "coupling"):
+        fetched[name].wait()
     for j in range(blocks):
         mask = map_ref[0, j].astype(F32)
         masked_ref[j] = (coupling_ref[j].astype(F32) * mask).astype(BF16)
@@ -354,8 +387,11 @@
         target = centering * every[2:3] / (2.0 * entries)
         return 1.0 / (1.0 + dual_rms), step / (1.0 + primal_rms), step * target
 
+    for name in ("numer", "denom", "linear", "cost"):
+        fetched[name].wait()
     step = step_of(0)
     gap_row, square_row = residuals(step, True)
+    fetched["load"].wait()
     wait_for(recv_sem.at[START], spans[START])
     per_zone = jnp.sum(zc_ref[...], axis=0)
 
@@ -520,7 +556,7 @@
         entries = float(n_s * rows * width * n_g)
         zone_entries = float(n_s * rows * zones)
         vmem = pl.BlockSpec(memory_space=pltpu.VMEM)
-        smem = pl.BlockSpec(memory_space=pltpu.SMEM)
+        hbm = pl.BlockSpec(memory_space=pltpu.HBM)
         state = pltpu.VMEM((rows, width), F32)
         share = rows // n_g
         dispatch, prices, plan = pl.pallas_call(
@@ -537,9 +573,19 @@
                 jax.ShapeDtypeStruct((rows, zones), F32),
                 jax.ShapeDtypeStruct((periods, width), F32),
             ),
-            in_specs=[vmem] * 6 + [smem, vmem, smem, smem],
+            in_specs=[hbm] * 10,
             out_specs=(vmem, vmem, vmem),
             scratch_shapes=[
+                pltpu.VMEM((rows, zones), F32),
+                pltpu.VMEM((periods, width), F32),
+                pltpu.VMEM((width,), F32),
+                pltpu.VMEM((width,), F32),
+                pltpu.VMEM((blocks, tile, tile), BF16),
+                pltpu.VMEM((blocks, tile, tile), BF16),
+                pltpu.SMEM(block_map.shape, jnp.int32),
+                pltpu.VMEM((width,), jnp.int32),
+                pltpu.SMEM(step_numer.shape, jnp.int32),
+                pltpu.SMEM(step_denom.shape, jnp.int32),
                 state,
                 state,
                 state,
@@ -569,6 +615,7 @@
                 pltpu.SemaphoreType.DMA((7,)),
                 pltpu.SemaphoreType.DMA((7,)),
                 pltpu.SemaphoreType.DMA((2,)),
+                pltpu.SemaphoreType.DMA((10,)),
             ],
             compiler_params=pltpu.CompilerParams(collective_id=0, has_side_effects=True),
         )(

time: 107 us -> 106 us (level)
    pallas_call x1, Pallas kernels: 102 us -> 101 us  [local(): pl.pallas_call(functools.partial(kernel, scen_dims, gen_dims, entries, zo...]
where the time goes in v3:
time: 106 us
  Pallas kernels  101 us (95%)
  local copies, waits for them, and re-layouts  3.86 us (4%)
    pallas_call x1, Pallas kernels, local(): pl.pallas_call(functools.partial(kernel, scen_dims, gen_dims, entries, zo...  101 us
    unnamed x7, local copies, waits for them, and re-layouts  3.86 us

profile of v3, /device:TPU:1, one launch (start us, length us, event | category | flops | bytes accessed | tf_op | source)
XLA Modules:
  0.0 105.6 jit_solution(14911382904889058830)
XLA Ops:
  0.6 101.1 %shard_map.121 = (f32[256,1280]{1,0:T(8,128)}, f32[256,256]{1,0:T(8,128)}, f32[16,1280]{1,0:T(8,128)}) custom-call(f32[256,256]{1,0:T(8,128)} %bitcast.7, f32[16,1280]{1,0:T(8,128)} %linear_hbm.1, f32[1280]{0:T(1024)} %diag_hbm.1, f32[1280]{0:T(1024)} %cap_hbm.1, bf16[5,256,256]{2,1,0:T(8,128)(2,1)} %cost_hbm.1, bf16[5,256,256]{2,1,0:T(8,128)(2,1)} %bitcast.5, ...), custom_call_target="tpu_custom_call" | custom-call | tf_op jit(solution)/shard_map/pallas_call | solution.py:562
  101.7 0.0 copy-start
  101.7 0.0 copy-start.1
  101.7 2.5 %copy.16 = f32[16,16,1280]{2,1,0:T(8,128)} copy(f32[16,16,1280]{2,1,0:T(8,128)} %bitcast.4) | data formatting | bytes 2621440
  104.2 0.0 copy-done
  104.2 0.7 copy.17
  104.9 0.0 copy-done.1
  104.9 0.6 copy.18
Async XLA Ops:
  101.7 2.5 %copy-start = (f32[256,256]{1,0:T(8,128)S(1)}, f32[256,256]{1,0:T(8,128)}, u32[]{:S(2)}) copy-start(f32[256,256]{1,0:T(8,128)} %get-tuple-element.7) | copy-start | bytes 786436
  101.7 3.2 %copy-start.1 = (f32[16,1280]{1,0:T(8,128)S(1)}, f32[16,1280]{1,0:T(8,128)}, u32[]{:S(2)}) copy-start(f32[16,1280]{1,0:T(8,128)} %get-tuple-element.14) | copy-start | bytes 245764

commit v4 on v3

--- a/solution.py
+++ b/solution.py
@@ -67,6 +67,9 @@
     zone_hbm,
     numer_hbm,
     denom_hbm,
+    x_out,
+    prices_out,
+    plan_out,
     x_ref,
     prices_ref,
     plan_ref,
@@ -105,11 +108,13 @@
     nr_ref,
     fs_ref,
     fr_ref,
+    wide_ref,
     all_ref,
     send_sem,
     recv_sem,
     far_sem,
     in_sem,
+    out_sem,
 ):
     me_s = lax.axis_index("scen")
     me_g = lax.axis_index("gen")
@@ -201,7 +206,7 @@
     def wait_for(sem, span):
         pltpu.make_async_copy(span, span, sem).wait()
 
-    ZONE, COLUMN, PLAN, IMB, NEAR, FAR, START = range(7)
+    ZONE, COLUMN, PLAN, IMB, NEAR, FAR, START, WIDE = range(8)
     spans = {
         ZONE: zr_ref,
         COLUMN: cr_ref,
@@ -210,6 +215,7 @@
         NEAR: nr_ref,
         FAR: fr_ref.at[0],
         START: zc_ref.at[pl.ds(0, n_g - 1)],
+        WIDE: wide_ref,
     }
 
     def level(s, shape):
@@ -262,6 +268,7 @@
     paid_ref[...] = jnp.zeros_like(paid_ref)
     cs_ref[...] = jnp.zeros_like(cs_ref)
     ns_ref[...] = jnp.zeros_like(ns_ref)
+    fs_ref[...] = jnp.zeros_like(fs_ref)
     pg_ref[...] = jnp.zeros_like(pg_ref)
 
     def residuals(step, first):
@@ -313,20 +320,26 @@
             square_row = square_row + fold(square)
         return gap_row, square_row
 
-    def exchange(k, first):
+    def lump():
+        lumped = jnp.zeros((periods, zones), F32)
+        for s in range(scens):
+            lumped = lumped + imb_ref[s * periods : (s + 1) * periods, :]
+        both = jnp.concatenate(two_parts(lumped), axis=0)
+        for j in range(blocks):
+            found = jnp.dot(both, onehot_ref[:, columns(j)], preferred_element_type=F32)
+            more_ref[:, columns(j)] = found[:periods] + found[periods:]
+
+    def keep_sums(every):
+        all_ref[...] = jnp.broadcast_to(jnp.sum(every, axis=1, keepdims=True), (4, LANES))
+
+    def exchange(k):
+        send(NEAR, line_to, lambda t: ns_ref, lambda slot: nr_ref.at[slot])
         send(
-            NEAR,
-            line_to,
-            lambda t: ns_ref,
-            lambda slot: nr_ref.at[slot],
+            PLAN,
+            scen_to,
+            lambda t: pg_ref.at[pl.ds(own, plan_rows)],
+            lambda slot: pg_ref.at[pl.ds(own, plan_rows)],
         )
-        if not first:
-            send(
-                PLAN,
-                scen_to,
-                lambda t: pg_ref.at[pl.ds(own, plan_rows)],
-                lambda slot: pg_ref.at[pl.ds(own, plan_rows)],
-            )
         wait_for(recv_sem.at[NEAR], spans[NEAR])
         near = ns_ref[...]
         for slot in range(depth - 1):
@@ -340,45 +353,37 @@
             lambda slot: fr_ref.at[turn, slot],
             far_sem.at[turn],
         )
-        if not first:
-            wait_for(recv_sem.at[IMB], spans[IMB])
-        lumped = jnp.zeros((periods, zones), F32)
-        for s in range(scens):
-            lumped = lumped + imb_ref[s * periods : (s + 1) * periods, :]
-        both = jnp.concatenate(two_parts(lumped), axis=0)
+        wait_for(recv_sem.at[IMB], spans[IMB])
+        lump()
+        wait_for(recv_sem.at[PLAN], spans[PLAN])
         for j in range(blocks):
-            found = jnp.dot(both, onehot_ref[:, columns(j)], preferred_element_type=F32)
-            more_ref[:, columns(j)] = found[:periods] + found[periods:]
-        if not first:
-            wait_for(recv_sem.at[PLAN], spans[PLAN])
-            for j in range(blocks):
-                pieces = [
-                    jnp.concatenate(
-                        [
-                            pg_ref[
-                                pl.ds(h * 8 * plan_rows + j * tiles + t, 8, stride=plan_rows), :
-                            ]
-                            for t in range(tiles)
-                        ],
-                        axis=1,
-                    )
-                    for h in range(halves)
-                ]
-                plan = jnp.concatenate(pieces, axis=0)
-                plan_ref[:, columns(j)] = plan
-                twice = penalty * plan
-
-                def settle(s, none):
-                    here = (scen_rows(s), columns(j))
-                    res_ref[here] = (res_ref[here] - twice) * inv_ref[here]
-                    return none
-
-                lax.fori_loop(0, scens, settle, 0, unroll=4)
+            pieces = [
+                jnp.concatenate(
+                    [
+                        pg_ref[
+                            pl.ds(h * 8 * plan_rows + j * tiles + t, 8, stride=plan_rows), :
+                        ]
+                        for t in range(tiles)
+                    ],
+                    axis=1,
+                )
+                for h in range(halves)
+            ]
+            plan = jnp.concatenate(pieces, axis=0)
+            plan_ref[:, columns(j)] = plan
+            twice = penalty * plan
+
+            def settle(s, none):
+                here = (scen_rows(s), columns(j))
+                res_ref[here] = (res_ref[here] - twice) * inv_ref[here]
+                return none
+
+            lax.fori_loop(0, scens, settle, 0, unroll=4)
         wait_for(far_sem.at[turn], spans[FAR])
         every = fs_ref[...]
         for slot in range(n_g * sides - 1):
             every = every + fr_ref[turn, slot]
-        all_ref[...] = jnp.broadcast_to(jnp.sum(every, axis=1, keepdims=True), (4, LANES))
+        keep_sums(every)
 
     def scalars(step):
         every = all_ref[:, 0:1]
@@ -391,23 +396,35 @@
         fetched[name].wait()
     step = step_of(0)
     gap_row, square_row = residuals(step, True)
+    fs_ref[0:1, :] = square_row
+    fs_ref[2:3, :] = gap_row
+    send(FAR, plane_to, lambda t: fs_ref, lambda slot: fr_ref.at[0, slot], far_sem.at[0])
     fetched["load"].wait()
     wait_for(recv_sem.at[START], spans[START])
     per_zone = jnp.sum(zc_ref[...], axis=0)
 
-    def imbalances(s, none):
+    def imbalances(s, square):
         here = scen_rows(s)
-        imb_ref[here, :] = level(s, (periods, zones)) * per_zone * zone_scale - load_ref[here, :]
-        return none
-
-    lax.fori_loop(0, scens, imbalances, 0, unroll=2)
-    imbalance = imb_ref[mine, :]
-    ns_ref[0:1, :] = square_row
-    ns_ref[1:2, :] = fold(imbalance * imbalance)
-    ns_ref[2:3, :] = gap_row
-    exchange(0, True)
-    wait_for(send_sem.at[START], spans[START])
-    for kind in (NEAR, FAR):
+        value = level(s, (periods, zones)) * per_zone * zone_scale - load_ref[here, :]
+        imb_ref[here, :] = value
+        return square + value * value
+
+    square = lax.fori_loop(0, scens, imbalances, jnp.zeros((periods, zones), F32), unroll=2)
+    primal_row = fold(square)
+    lump()
+    wait_for(far_sem.at[0], spans[FAR])
+    every = fs_ref[...]
+    for slot in range(n_g * sides - 1):
+        every = every + fr_ref[0, slot]
+    ns_ref[...] = every * (1.0 / sides)
+    ns_ref[1:2, :] = primal_row
+    send(WIDE, scen_to, lambda t: ns_ref, lambda slot: wide_ref.at[slot])
+    wait_for(recv_sem.at[WIDE], spans[WIDE])
+    every = ns_ref[...]
+    for slot in range(n_s - 1):
+        every = every + wide_ref[slot]
+    keep_sums(every)
+    for kind in (START, FAR, WIDE):
         wait_for(send_sem.at[kind], spans[kind])
 
     def iteration(k, carry):
@@ -507,15 +524,16 @@
         term = (2.0 * penalty) * plan * ((penalty / 2.0) * total_scen * plan - rest)
         ns_ref[0:1, :] = square_row + jnp.sum(term, axis=0, keepdims=True)
         pg_ref[pl.ds(own, lane_tiles), :] = plan
-        exchange(k + 1, False)
+        exchange(k + 1)
         for kind in (ZONE, COLUMN, PLAN, IMB, NEAR, FAR):
             wait_for(send_sem.at[kind], spans[kind])
         return carry
 
     lax.fori_loop(0, ITERS - 1, iteration, 0)
 
+    leaving = [pltpu.make_async_copy(plan_ref, plan_out, out_sem.at[0])]
+    leaving[0].start()
     shrink, pay, _ = scalars(step_of(ITERS - 1))
-    prices_ref[...] += pay * imb_ref[...]
     for j in range(blocks):
         cap = cap_ref[:, columns(j)]
         lowest = 0.02 * cap
@@ -527,6 +545,17 @@
             return none
 
         lax.fori_loop(0, scens, finish, 0, unroll=4)
+        copy = pltpu.make_async_copy(
+            x_ref.at[:, columns(j)], x_out.at[:, columns(j)], out_sem.at[1 + j]
+        )
+        copy.start()
+        leaving.append(copy)
+    prices_ref[...] += pay * imb_ref[...]
+    copy = pltpu.make_async_copy(prices_ref, prices_out, out_sem.at[1 + blocks])
+    copy.start()
+    leaving.append(copy)
+    for copy in leaving:
+        copy.wait()
 
 
 def solution(mesh):
@@ -555,7 +584,6 @@
         plan_rows = -(-lane_tiles // 8) * 8
         entries = float(n_s * rows * width * n_g)
         zone_entries = float(n_s * rows * zones)
-        vmem = pl.BlockSpec(memory_space=pltpu.VMEM)
         hbm = pl.BlockSpec(memory_space=pltpu.HBM)
         state = pltpu.VMEM((rows, width), F32)
         share = rows // n_g
@@ -574,8 +602,11 @@
                 jax.ShapeDtypeStruct((periods, width), F32),
             ),
             in_specs=[hbm] * 10,
-            out_specs=(vmem, vmem, vmem),
+            out_specs=(hbm, hbm, hbm),
             scratch_shapes=[
+                state,
+                pltpu.VMEM((rows, zones), F32),
+                pltpu.VMEM((periods, width), F32),
                 pltpu.VMEM((rows, zones), F32),
                 pltpu.VMEM((periods, width), F32),
                 pltpu.VMEM((width,), F32),
@@ -611,11 +642,13 @@
                 pltpu.VMEM((scen_dims[0] - 1, 4, LANES), F32),
                 pltpu.VMEM((4, LANES), F32),
                 pltpu.VMEM((2, n_g * scen_dims[1] - 1, 4, LANES), F32),
+                pltpu.VMEM((n_s - 1, 4, LANES), F32),
                 pltpu.VMEM((4, LANES), F32),
-                pltpu.SemaphoreType.DMA((7,)),
-                pltpu.SemaphoreType.DMA((7,)),
+                pltpu.SemaphoreType.DMA((8,)),
+                pltpu.SemaphoreType.DMA((8,)),
                 pltpu.SemaphoreType.DMA((2,)),
                 pltpu.SemaphoreType.DMA((10,)),
+                pltpu.SemaphoreType.DMA((cost_tiles.shape[0] + 2,)),
             ],
             compiler_params=pltpu.CompilerParams(collective_id=0, has_side_effects=True),
         )(

time: 106 us -> 105 us (level)
  no operation moved by 1% of the time
where the time goes in v4:
time: 105 us
  Pallas kernels  100 us (95%)
  local copies, waits for them, and re-layouts  3.86 us (4%)
    pallas_call x1, Pallas kernels, local(): pl.pallas_call(functools.partial(kernel, scen_dims, gen_dims, entries, zo...  100 us
    unnamed x7, local copies, waits for them, and re-layouts  3.86 us

profile of v4, /device:TPU:1, one launch (start us, length us, event | category | flops | bytes accessed | tf_op | source)
XLA Modules:
  0.0 105.0 jit_solution(8494041745521246312)
XLA Ops:
  0.6 100.5 %shard_map.121 = (f32[256,1280]{1,0:T(8,128)}, f32[256,256]{1,0:T(8,128)}, f32[16,1280]{1,0:T(8,128)}) custom-call(f32[256,256]{1,0:T(8,128)} %bitcast.7, f32[16,1280]{1,0:T(8,128)} %linear_hbm.1, f32[1280]{0:T(1024)} %diag_hbm.1, f32[1280]{0:T(1024)} %cap_hbm.1, bf16[5,256,256]{2,1,0:T(8,128)(2,1)} %cost_hbm.1, bf16[5,256,256]{2,1,0:T(8,128)(2,1)} %bitcast.5, ...), custom_call_target="tpu_custom_call" | custom-call | tf_op jit(solution)/shard_map/pallas_call | solution.py:590
  101.1 0.0 copy-start
  101.1 0.0 copy-start.1
  101.1 2.5 %copy.16 = f32[16,16,1280]{2,1,0:T(8,128)} copy(f32[16,16,1280]{2,1,0:T(8,128)} %bitcast.4) | data formatting | bytes 2621440
  103.7 0.0 copy-done
  103.7 0.7 copy.17
  104.4 0.0 copy-done.1
  104.4 0.6 copy.18
Async XLA Ops:
  101.1 2.5 %copy-start = (f32[256,256]{1,0:T(8,128)S(1)}, f32[256,256]{1,0:T(8,128)}, u32[]{:S(2)}) copy-start(f32[256,256]{1,0:T(8,128)} %get-tuple-element.7) | copy-start | bytes 786436
  101.1 3.2 %copy-start.1 = (f32[16,1280]{1,0:T(8,128)S(1)}, f32[16,1280]{1,0:T(8,128)}, u32[]{:S(2)}) copy-start(f32[16,1280]{1,0:T(8,128)} %get-tuple-element.14) | copy-start | bytes 245764

commit v5 on v4

--- a/solution.py
+++ b/solution.py
@@ -247,9 +247,6 @@
         start = start + jnp.dot(both, turned, preferred_element_type=F32)
     zc_ref[me_g] = start[0:1] + start[8:9]
 
-    pl.semaphore_wait(barrier, len(greeted))
-    send(START, gen_to, lambda t: zc_ref.at[me_g], lambda slot: zc_ref.at[me_g])
-
     for name in ("map", "coupling"):
         fetched[name].wait()
     for j in range(blocks):
@@ -398,6 +395,8 @@
     gap_row, square_row = residuals(step, True)
     fs_ref[0:1, :] = square_row
     fs_ref[2:3, :] = gap_row
+    pl.semaphore_wait(barrier, len(greeted))
+    send(START, gen_to, lambda t: zc_ref.at[me_g], lambda slot: zc_ref.at[me_g])
     send(FAR, plane_to, lambda t: fs_ref, lambda slot: fr_ref.at[0, slot], far_sem.at[0])
     fetched["load"].wait()
     wait_for(recv_sem.at[START], spans[START])
@@ -411,7 +410,6 @@
 
     square = lax.fori_loop(0, scens, imbalances, jnp.zeros((periods, zones), F32), unroll=2)
     primal_row = fold(square)
-    lump()
     wait_for(far_sem.at[0], spans[FAR])
     every = fs_ref[...]
     for slot in range(n_g * sides - 1):
@@ -419,6 +417,7 @@
     ns_ref[...] = every * (1.0 / sides)
     ns_ref[1:2, :] = primal_row
     send(WIDE, scen_to, lambda t: ns_ref, lambda slot: wide_ref.at[slot])
+    lump()
     wait_for(recv_sem.at[WIDE], spans[WIDE])
     every = ns_ref[...]
     for slot in range(n_s - 1):
@@ -555,6 +554,29 @@
     copy.start()
     leaving.append(copy)
     for copy in leaving:
+        copy.wait()
+
+
+def relay(x_in, prices_in, plan_in, x_out, prices_out, plan_out, x, prices, plan, came, went):
+    pieces = []
+    rows = x.shape[0] // 4
+    for part in range(4):
+        here = pl.ds(part * rows, rows)
+        pieces.append((x_in.at[here], x.at[here], x_out.at[here]))
+    pieces.append((prices_in, prices, prices_out))
+    pieces.append((plan_in, plan, plan_out))
+    coming = [
+        pltpu.make_async_copy(source, held, came.at[i]) for i, (source, held, _) in enumerate(pieces)
+    ]
+    going = [
+        pltpu.make_async_copy(held, place, went.at[i]) for i, (_, held, place) in enumerate(pieces)
+    ]
+    for copy in coming:
+        copy.start()
+    for first, second in zip(coming, going):
+        first.wait()
+        second.start()
+    for copy in going:
         copy.wait()
 
 
@@ -663,6 +685,15 @@
             step_numer,
             step_denom,
         )
+        results = (dispatch, prices, plan)
+        dispatch, prices, plan = pl.pallas_call(
+            relay,
+            out_shape=tuple(jax.ShapeDtypeStruct(r.shape, r.dtype) for r in results),
+            in_specs=[hbm] * 3,
+            out_specs=(hbm, hbm, hbm),
+            scratch_shapes=[pltpu.VMEM(r.shape, r.dtype) for r in results]
+            + [pltpu.SemaphoreType.DMA((6,)), pltpu.SemaphoreType.DMA((6,))],
+        )(*results)
         return dispatch.reshape(scens, periods, width), prices.reshape(scens, periods, zones), plan
 
     return jax.shard_map(

time: 105 us -> 102 us (0.971)
  local copies, waits for them, and re-layouts: 3.86 us -> 0 us
    unnamed x7 -> x0, local copies, waits for them, and re-layouts: 3.86 us -> none
    pallas_call x0 -> x1, Pallas kernels: none -> 2.23 us  [local(): pl.pallas_call(relay, out_shape=tuple((jax.ShapeDtypeStruct(r.shape, r.dt...]
    pallas_call x1, Pallas kernels: 100 us -> 98.8 us  [local(): pl.pallas_call(functools.partial(kernel, scen_dims, gen_dims, entries, zo...]
where the time goes in v5:
time: 102 us
  Pallas kernels  101 us (99%)
    pallas_call x1, Pallas kernels, local(): pl.pallas_call(functools.partial(kernel, scen_dims, gen_dims, entries, zo...  98.8 us
    pallas_call x1, Pallas kernels, local(): pl.pallas_call(relay, out_shape=tuple((jax.ShapeDtypeStruct(r.shape, r.dt...  2.23 us

profile of v5, /device:TPU:1, one launch (start us, length us, event | category | flops | bytes accessed | tf_op | source)
XLA Modules:
  0.0 101.6 jit_solution(908474015279667231)
XLA Ops:
  0.6 98.8 %shard_map.121 = (f32[256,1280]{1,0:T(8,128)}, f32[256,256]{1,0:T(8,128)}, f32[16,1280]{1,0:T(8,128)}) custom-call(f32[256,256]{1,0:T(8,128)} %bitcast.5, f32[16,1280]{1,0:T(8,128)} %linear_hbm.1, f32[1280]{0:T(1024)} %diag_hbm.1, f32[1280]{0:T(1024)} %cap_hbm.1, bf16[5,256,256]{2,1,0:T(8,128)(2,1)} %cost_hbm.1, bf16[5,256,256]{2,1,0:T(8,128)(2,1)} %bitcast.4, ...), custom_call_target="tpu_custom_call" | custom-call | tf_op jit(solution)/shard_map/pallas_call | solution.py:612
  99.4 2.2 %shard_map.122 = (f32[256,1280]{1,0:T(8,128)}, f32[256,256]{1,0:T(8,128)}, f32[16,1280]{1,0:T(8,128)}) custom-call(f32[256,1280]{1,0:T(8,128)} %get-tuple-element.9.x_in, f32[256,256]{1,0:T(8,128)} %get-tuple-element.10.prices_in, f32[16,1280]{1,0:T(8,128)} %get-tuple-element.11.plan_in), custom_call_target="tpu_custom_call" | custom-call | tf_op jit(solution)/shard_map/pallas_call | solution.py:689

commit v6 on v4

--- a/solution.py
+++ b/solution.py
@@ -49,6 +49,13 @@
 def two_parts(value):
     high = value.astype(BF16)
     return high, (value - high.astype(F32)).astype(BF16)
+
+
+def rates(every, step, entries, zone_entries):
+    dual_rms = jnp.sqrt(every[0:1] / entries + epsilon)
+    primal_rms = jnp.sqrt(every[1:2] / zone_entries + epsilon)
+    target = centering * every[2:3] / (2.0 * entries)
+    return 1.0 / (1.0 + dual_rms), step / (1.0 + primal_rms), step * target
 
 
 def kernel(
@@ -68,8 +75,11 @@
     numer_hbm,
     denom_hbm,
     x_out,
+    move_out,
     prices_out,
+    imb_out,
     plan_out,
+    all_out,
     x_ref,
     prices_ref,
     plan_ref,
@@ -247,9 +257,6 @@
         start = start + jnp.dot(both, turned, preferred_element_type=F32)
     zc_ref[me_g] = start[0:1] + start[8:9]
 
-    pl.semaphore_wait(barrier, len(greeted))
-    send(START, gen_to, lambda t: zc_ref.at[me_g], lambda slot: zc_ref.at[me_g])
-
     for name in ("map", "coupling"):
         fetched[name].wait()
     for j in range(blocks):
@@ -379,18 +386,30 @@
                 return none
 
             lax.fori_loop(0, scens, settle, 0, unroll=4)
+        leaving = [
+            pltpu.make_async_copy(source, place, out_sem.at[i])
+            for i, (source, place) in enumerate(
+                (
+                    (x_ref, x_out),
+                    (res_ref, move_out),
+                    (prices_ref, prices_out),
+                    (imb_ref, imb_out),
+                    (plan_ref, plan_out),
+                )
+            )
+        ]
+        for copy in leaving:
+            copy.start()
         wait_for(far_sem.at[turn], spans[FAR])
         every = fs_ref[...]
         for slot in range(n_g * sides - 1):
             every = every + fr_ref[turn, slot]
         keep_sums(every)
+        for copy in leaving:
+            copy.wait()
 
     def scalars(step):
-        every = all_ref[:, 0:1]
-        dual_rms = jnp.sqrt(every[0:1] / entries + epsilon)
-        primal_rms = jnp.sqrt(every[1:2] / zone_entries + epsilon)
-        target = centering * every[2:3] / (2.0 * entries)
-        return 1.0 / (1.0 + dual_rms), step / (1.0 + primal_rms), step * target
+        return rates(all_ref[:, 0:1], step, entries, zone_entries)
 
     for name in ("numer", "denom", "linear", "cost"):
         fetched[name].wait()
@@ -398,6 +417,8 @@
     gap_row, square_row = residuals(step, True)
     fs_ref[0:1, :] = square_row
     fs_ref[2:3, :] = gap_row
+    pl.semaphore_wait(barrier, len(greeted))
+    send(START, gen_to, lambda t: zc_ref.at[me_g], lambda slot: zc_ref.at[me_g])
     send(FAR, plane_to, lambda t: fs_ref, lambda slot: fr_ref.at[0, slot], far_sem.at[0])
     fetched["load"].wait()
     wait_for(recv_sem.at[START], spans[START])
@@ -411,7 +432,6 @@
 
     square = lax.fori_loop(0, scens, imbalances, jnp.zeros((periods, zones), F32), unroll=2)
     primal_row = fold(square)
-    lump()
     wait_for(far_sem.at[0], spans[FAR])
     every = fs_ref[...]
     for slot in range(n_g * sides - 1):
@@ -419,6 +439,7 @@
     ns_ref[...] = every * (1.0 / sides)
     ns_ref[1:2, :] = primal_row
     send(WIDE, scen_to, lambda t: ns_ref, lambda slot: wide_ref.at[slot])
+    lump()
     wait_for(recv_sem.at[WIDE], spans[WIDE])
     every = ns_ref[...]
     for slot in range(n_s - 1):
@@ -531,30 +552,80 @@
 
     lax.fori_loop(0, ITERS - 1, iteration, 0)
 
-    leaving = [pltpu.make_async_copy(plan_ref, plan_out, out_sem.at[0])]
-    leaving[0].start()
-    shrink, pay, _ = scalars(step_of(ITERS - 1))
-    for j in range(blocks):
-        cap = cap_ref[:, columns(j)]
-        lowest = 0.02 * cap
-        highest = 0.98 * cap
-
-        def finish(s, none):
-            here = (scen_rows(s), columns(j))
-            x_ref[here] = jnp.clip(x_ref[here] - res_ref[here] * shrink, lowest, highest)
+    copy = pltpu.make_async_copy(all_ref, all_out, out_sem.at[5])
+    copy.start()
+    copy.wait()
+
+
+def finish(
+    entries,
+    zone_entries,
+    last,
+    x_in,
+    move_in,
+    prices_in,
+    imb_in,
+    plan_in,
+    all_in,
+    cap_in,
+    numer_ref,
+    denom_ref,
+    x_out,
+    prices_out,
+    plan_out,
+    x,
+    move,
+    prices,
+    imb,
+    plan,
+    every,
+    cap_flat,
+    came,
+    went,
+):
+    parts = 4
+    rows = x.shape[0] // parts
+    small = [(all_in, every), (cap_in, cap_flat)]
+    for part in range(parts):
+        here = pl.ds(part * rows, rows)
+        small += [(x_in.at[here], x.at[here]), (move_in.at[here], move.at[here])]
+    small += [(prices_in, prices), (imb_in, imb), (plan_in, plan)]
+    coming = [pltpu.make_async_copy(a, b, came.at[i]) for i, (a, b) in enumerate(small)]
+    for copy in coming:
+        copy.start()
+    coming[0].wait()
+    coming[1].wait()
+    numer = jnp.full((1, 1), numer_ref[last], jnp.int32).astype(F32)
+    step = numer / jnp.full((1, 1), denom_ref[last], jnp.int32).astype(F32)
+    shrink, pay, _ = rates(every[:, 0:1], step, entries, zone_entries)
+    cap = cap_flat[...].reshape(1, x.shape[1])
+    lowest = 0.02 * cap
+    highest = 0.98 * cap
+    going = []
+
+    def leave(source, place):
+        copy = pltpu.make_async_copy(source, place, went.at[len(going)])
+        copy.start()
+        going.append(copy)
+
+    for part in range(parts):
+        coming[2 + 2 * part].wait()
+        coming[3 + 2 * part].wait()
+
+        def clipped(i, none):
+            here = pl.ds(pl.multiple_of(part * rows + i * 8, 8), 8)
+            x[here, :] = jnp.clip(x[here, :] - move[here, :] * shrink, lowest, highest)
             return none
 
-        lax.fori_loop(0, scens, finish, 0, unroll=4)
-        copy = pltpu.make_async_copy(
-            x_ref.at[:, columns(j)], x_out.at[:, columns(j)], out_sem.at[1 + j]
-        )
-        copy.start()
-        leaving.append(copy)
-    prices_ref[...] += pay * imb_ref[...]
-    copy = pltpu.make_async_copy(prices_ref, prices_out, out_sem.at[1 + blocks])
-    copy.start()
-    leaving.append(copy)
-    for copy in leaving:
+        lax.fori_loop(0, rows // 8, clipped, 0, unroll=2)
+        here = pl.ds(part * rows, rows)
+        leave(x.at[here], x_out.at[here])
+    for copy in coming[2 + 2 * parts :]:
+        copy.wait()
+    leave(plan, plan_out)
+    prices[...] += pay * imb[...]
+    leave(prices, prices_out)
+    for copy in going:
         copy.wait()
 
 
@@ -587,7 +658,7 @@
         hbm = pl.BlockSpec(memory_space=pltpu.HBM)
         state = pltpu.VMEM((rows, width), F32)
         share = rows // n_g
-        dispatch, prices, plan = pl.pallas_call(
+        results = pl.pallas_call(
             functools.partial(
                 kernel,
                 scen_dims,
@@ -598,11 +669,14 @@
             ),
             out_shape=(
                 jax.ShapeDtypeStruct((rows, width), F32),
+                jax.ShapeDtypeStruct((rows, width), F32),
+                jax.ShapeDtypeStruct((rows, zones), F32),
                 jax.ShapeDtypeStruct((rows, zones), F32),
                 jax.ShapeDtypeStruct((periods, width), F32),
+                jax.ShapeDtypeStruct((4, LANES), F32),
             ),
             in_specs=[hbm] * 10,
-            out_specs=(hbm, hbm, hbm),
+            out_specs=(hbm,) * 6,
             scratch_shapes=[
                 state,
                 pltpu.VMEM((rows, zones), F32),
@@ -648,7 +722,7 @@
                 pltpu.SemaphoreType.DMA((8,)),
                 pltpu.SemaphoreType.DMA((2,)),
                 pltpu.SemaphoreType.DMA((10,)),
-                pltpu.SemaphoreType.DMA((cost_tiles.shape[0] + 2,)),
+                pltpu.SemaphoreType.DMA((6,)),
             ],
             compiler_params=pltpu.CompilerParams(collective_id=0, has_side_effects=True),
         )(
@@ -663,6 +737,19 @@
             step_numer,
             step_denom,
         )
+        smem = pl.BlockSpec(memory_space=pltpu.SMEM)
+        dispatch, prices, plan = pl.pallas_call(
+            functools.partial(finish, entries, zone_entries, ITERS - 1),
+            out_shape=tuple(jax.ShapeDtypeStruct(results[i].shape, F32) for i in (0, 2, 4)),
+            in_specs=[hbm] * 7 + [smem] * 2,
+            out_specs=(hbm, hbm, hbm),
+            scratch_shapes=[pltpu.VMEM(r.shape, r.dtype) for r in results]
+            + [
+                pltpu.VMEM((width,), F32),
+                pltpu.SemaphoreType.DMA((13,)),
+                pltpu.SemaphoreType.DMA((6,)),
+            ],
+        )(*results, capacity, step_numer, step_denom)
         return dispatch.reshape(scens, periods, width), prices.reshape(scens, periods, zones), plan
 
     return jax.shard_map(

time: 105 us -> 102 us (0.971)
  local copies, waits for them, and re-layouts: 3.86 us -> 0 us
    unnamed x7 -> x0, local copies, waits for them, and re-layouts: 3.86 us -> none
    pallas_call x0 -> x1, Pallas kernels: none -> 3.46 us  [local(): pl.pallas_call(functools.partial(finish, entries, zone_entries, ITERS - 1...]
    pallas_call x1, Pallas kernels: 100 us -> 97.8 us  [local(): pl.pallas_call(functools.partial(kernel, scen_dims, gen_dims, entries, zo...]
where the time goes in v6:
time: 102 us
  Pallas kernels  101 us (99%)
    pallas_call x1, Pallas kernels, local(): pl.pallas_call(functools.partial(kernel, scen_dims, gen_dims, entries, zo...  97.8 us
    pallas_call x1, Pallas kernels, local(): pl.pallas_call(functools.partial(finish, entries, zone_entries, ITERS - 1...  3.46 us

profile of v6, /device:TPU:1, one launch (start us, length us, event | category | flops | bytes accessed | tf_op | source)
XLA Modules:
  0.0 101.9 jit_solution(6776481392134153635)
XLA Ops:
  0.6 97.8 %shard_map.121 = (f32[256,1280]{1,0:T(8,128)}, f32[256,1280]{1,0:T(8,128)}, f32[256,256]{1,0:T(8,128)}, f32[256,256]{1,0:T(8,128)}, f32[16,1280]{1,0:T(8,128)}, /*index=5*/f32[4,128]{1,0:T(4,128)}) custom-call(f32[256,256]{1,0:T(8,128)} %bitcast.5, f32[16,1280]{1,0:T(8,128)} %linear_hbm.1, f32[1280]{0:T(1024)} %diag_hbm.1, f32[1280]{0:T(1024)} %cap_in.1, ...), custom_call_target="tpu_custom_call" | custom-call | tf_op jit(solution)/shard_map/pallas_call | solution.py:661
  98.4 3.5 %shard_map.122 = (f32[256,1280]{1,0:T(8,128)}, f32[256,256]{1,0:T(8,128)}, f32[16,1280]{1,0:T(8,128)}) custom-call(f32[256,1280]{1,0:T(8,128)} %get-tuple-element.12.x_in, f32[256,1280]{1,0:T(8,128)} %get-tuple-element.13.move_in, f32[256,256]{1,0:T(8,128)} %get-tuple-element.14.prices_in, f32[256,256]{1,0:T(8,128)} %get-tuple-element.15.imb_in, ...), custom_call_target="tpu_custom_call" | custom-call | tf_op jit(solution)/shard_map/pallas_call | solution.py:741
